TPU v7x, 256 devices: a whole 4x4x8 slice. The times are simulated.
256 devices in a mesh: expert: 8 (over z_lo, y), shard: 32 (over z_hi, x, core).
Axes of the slice: x: 4, y: 4, z: 8 (z_hi: 4, z_lo: 2; z = z_hi * 2 + z_lo), core: 2. Of those that a mesh axis runs over, the one named last changes fastest.
Arguments:
- tokens: bfloat16 [2048, 6144], P(('expert', 'shard')), may hold values from -6 to 6
- norm_gain: float32 [6144], replicated, may hold values from 0.5 to 1.5
- routes: int32 [2048, 2], P(('expert', 'shard')), may hold values from 0 to 7, all different within a row; in each aligned block of 8 rows (0 to 7, 8 to 15, ...) at most 4 rows name the same one
- gate_weights: float32 [2048, 2], P(('expert', 'shard')), may hold values from 0.2 to 1
- capacity: int32 [8], replicated, may hold values from 2 to 4
- w_gate: bfloat16 [8, 6144, 8192], P('expert', None, 'shard'), may hold values from -0.078125 to 0.078125
- w_up: bfloat16 [8, 6144, 8192], P('expert', None, 'shard'), may hold values from -0.078125 to 0.078125
- w_down: bfloat16 [8, 8192, 6144], P('expert', 'shard'), may hold values from -0.0625 to 0.0625
Outputs:
- mixed_out: bfloat16 [2048, 6144], P(('expert', 'shard'))
Inputs may be any that keep to these rules, and one draw needn't show every extreme that they name: `routes`: each row names 2 different experts; among the rows of one device no expert is named by more than 4 rows.
All inputs are finite; a program needn't handle non-finite values.
Results may differ from a plain program's by a relative error of at most 0.019.
Values may be sent and summed in bfloat16 or wider, within the bound.
A program may use at most 128 MiB of HBM per device.

v0:
```python
import jax
import jax.numpy as jnp
from jax import lax
from jax.sharding import PartitionSpec as P


def laid_out(parts, dim):
    parts = jnp.moveaxis(parts, 0, dim)
    dims = parts.shape
    return parts.reshape(*dims[:dim], dims[dim] * dims[dim + 1], *dims[dim + 2 :])


def on_gathered_pieces(array, axis, dim, work, out_dim):
    width = array.shape[dim]
    pieces = jnp.split(array, 2, axis=dim) if width % 2 == 0 else [array]
    leading = jnp.arange(lax.axis_size(axis)) * width
    parts = [lax.all_gather(slab, axis) for slab in pieces]
    made = [jax.vmap(work)(b, leading + k * (width // len(pieces))) for k, b in enumerate(parts)]
    return laid_out(jnp.concatenate(made, axis=out_dim + 1), out_dim)


def rms_norm(tokens, norm_gain):
    widened = tokens.astype(jnp.float32)
    mean_square = jnp.mean(widened * widened, axis=-1, keepdims=True)
    return (widened * lax.rsqrt(mean_square + 1e-05) * norm_gain).astype(jnp.bfloat16)


def slot_ranks(blocked):
    equal_ids = blocked[:, :, None, :, None] == blocked[:, None, :, None, :]
    shared = jnp.any(equal_ids, axis=4).astype(jnp.int32)
    per_block = blocked.shape[1]
    positions = jnp.arange(per_block, dtype=jnp.int32)
    earlier = (positions[None, :] < positions[:, None]).astype(jnp.int32)
    return jnp.sum(shared * earlier[None, :, :, None], axis=2)


def on_device(tokens, norm_gain, routes, gate_weights, capacity, w_gate, w_up, w_down):
    normed = rms_norm(tokens, norm_gain)
    tok_count = tokens.shape[0]
    expert_count = capacity.shape[0]
    slot_depth = max(tok_count // 2, tok_count * routes.shape[1] // expert_count)
    slot_rank = slot_ranks(routes[None])[0]
    expert_ids = jnp.arange(expert_count, dtype=jnp.int32)
    is_expert = routes[:, :, None] == expert_ids
    limit_rows = jnp.sum(jnp.where(is_expert, capacity, 0), axis=-1)
    kept_mask = slot_rank < limit_rows
    slot_ids = jnp.arange(slot_depth, dtype=jnp.int32)
    matched = (
        is_expert[:, :, :, None]
        & (slot_rank[:, :, None, None] == slot_ids)
        & kept_mask[:, :, None, None]
    )
    picker = jnp.sum(matched.astype(jnp.float32), axis=1).astype(jnp.bfloat16)
    buffers = jnp.einsum("tej,td->ejd", picker, normed, preferred_element_type=jnp.float32).astype(
        jnp.bfloat16
    )
    combine = jnp.sum(jnp.where(matched, gate_weights[:, :, None, None], jnp.float32(0.0)), axis=1)
    gate_proj = w_gate[0]
    up_proj = w_up[0]
    down_proj = w_down[0]

    def expert_apply(slot_rows):
        row_shape = slot_rows.shape
        flat_rows = slot_rows.reshape(-1, row_shape[-1])
        gate_val = jnp.dot(flat_rows, gate_proj, preferred_element_type=jnp.float32)
        up_val = jnp.dot(flat_rows, up_proj, preferred_element_type=jnp.float32)
        hidden = (jax.nn.silu(gate_val) * up_val).astype(jnp.bfloat16)
        partial_out = jnp.dot(hidden, down_proj, preferred_element_type=jnp.float32)
        return partial_out.reshape(row_shape[:-1] + (down_proj.shape[1],))

    arrived = lax.all_to_all(buffers, "expert", split_axis=0, concat_axis=0, tiled=True)

    def project(piece_rows, start_row):
        return expert_apply(piece_rows)

    partial_value = on_gathered_pieces(arrived[None], "shard", 0, project, 0)
    summed = lax.psum_scatter(
        partial_value.astype(jnp.bfloat16), "shard", scatter_dimension=0, tiled=True
    ).astype(jnp.float32)
    outputs = summed[0].astype(jnp.bfloat16)
    returned = lax.all_to_all(outputs, "expert", split_axis=0, concat_axis=0, tiled=True)
    mixed_out = jnp.einsum("tej,ejd->td", combine, returned.astype(jnp.float32))
    return mixed_out.astype(jnp.bfloat16)


def solution(mesh):
    in_specs = (
        P(("expert", "shard"), None),
        P(),
        P(("expert", "shard"), None),
        P(("expert", "shard"), None),
        P(),
        P("expert", None, "shard"),
        P("expert", None, "shard"),
        P("expert", "shard", None),
    )
    out_specs = P(("expert", "shard"), None)
    return jax.shard_map(
        on_device, mesh=mesh, in_specs=in_specs, out_specs=out_specs, check_vma=False
    )
```

profile of v0, /device:TPU:1, one launch (start us, length us, event | category | flops | bytes accessed | tf_op | source)
XLA Modules:
  0.0 330.2 jit_solution(11966711729966981635)
XLA Ops:
  6.5 0.0 copy-start
  6.5 0.0 all-gather.3.cloned.1.call-start
  6.5 0.9 compare_reduce_fusion
  7.5 0.8 iota_compare_fusion
  8.3 1.1 fusion.14
  9.3 0.9 select_reduce_fusion.1
  10.2 0.1 select_reduce_fusion.2
  10.4 0.8 convert_reduce_fusion
  11.2 1.2 convolution_convert_fusion.1
  12.4 0.3 copy.37
  12.7 13.7 %all_to_all.10 = bf16[8,4,6144]{2,1,0:T(4,128)(2,1)} all-to-all(bf16[8,4,6144]{2,1,0:T(4,128)(2,1)S(1)} %copy.37), channel_id=1, replica_groups=mesh['expert'=8,'shard'=32] {'expert'}, dimensions={0} | all-to-all | bytes 786432 | tf_op jit(solution)/shard_map/all_to_all | solution.py:71
  26.5 0.0 all-gather.3.cloned.1.call-update
  26.5 0.0 reduce-scatter.2.cloned.1.call-start
  26.5 94.3 %all-gather.3.cloned.1.call-done = bf16[256,4,6144]{2,1,0:T(4,128)(2,1)} async-done(((bf16[8,4,6144]{2,1,0:T(4,128)(2,1)}), bf16[256,4,6144]{2,1,0:T(4,128)(2,1)}) %all-gather.3.cloned.1.call-update) | async-done | bytes 12582928 | tf_op jit(solution)/shard_map/all_gather | solution.py:17
  120.8 19.3 %reshape.67 = bf16[32,32,6144]{2,1,0:T(8,128)(2,1)} reshape(bf16[256,4,6144]{2,1,0:T(4,128)(2,1)} %all-gather.3.cloned.1.call-done) | data formatting | bytes 25165824 | tf_op jit(solution)/shard_map/vmap()/reshape | solution.py:64
  140.1 0.0 copy-start.1
  140.1 0.0 copy-start.2
  140.1 7.5 %fusion.4 = f32[32,32,256]{2,1,0:T(8,128)S(1)} fusion(bf16[32,32,6144]{2,1,0:T(8,128)(2,1)} %reshape.67, bf16[1,6144,256]{2,1,0:T(8,128)(2,1)} %param.13), kind=kOutput, calls=%fused_computation.7 | convolution fusion | flops 3221225472 | bytes 16777216 | tf_op jit(solution)/shard_map/vmap()/dot_general | solution.py:65
  147.6 1.5 copy-done.1
  149.2 0.9 copy-done.2
  150.1 4.2 %fusion.9 = bf16[32,32,256]{2,1,0:T(8,128)(2,1)} fusion(bf16[32,32,6144]{2,1,0:T(8,128)(2,1)S(1)} %copy-done.1, bf16[1,6144,256]{2,1,0:T(8,128)(2,1)S(1)} %copy-done.2, f32[32,32,256]{2,1,0:T(8,128)S(1)} %fusion.4), kind=kOutput, calls=%fused_computation.10 | convolution fusion | flops 3222798336 | bytes 17301504 | tf_op jit(solution)/shard_map/vmap()/dot_general | solution.py:66
  154.3 2.0 dot_general.20
  156.3 0.0 copy-done
  156.3 7.4 %convolution_convert_fusion = bf16[32,8,4,6144]{3,1,2,0:T(8,128)(2,1)} fusion(bf16[1,256,6144]{2,1,0:T(8,128)(2,1)S(1)} %copy-done, bf16[32,8,4,256]{3,2,1,0:T(4,128)(2,1)} %dot_general.20), kind=kOutput, calls=%fused_computation | convolution fusion | flops 3227516928 | bytes 16252928 | tf_op jit(solution)/shard_map/vmap()/dot_general | solution.py:68
  163.7 0.0 reduce-scatter.2.cloned.1.call-update
  163.7 146.6 %reduce-scatter.2.cloned.1.call-done = bf16[1,8,4,6144]{3,1,2,0:T(8,128)(2,1)} async-done(((bf16[32,8,4,6144]{3,1,2,0:T(8,128)(2,1)}), bf16[1,8,4,6144]{3,1,2,0:T(8,128)(2,1)}) %reduce-scatter.2.cloned.1.call-update) | async-done | bytes 393232 | tf_op jit(solution)/shard_map/reduce_scatter | solution.py:77
  310.3 1.3 copy.39
  311.6 10.7 %all_to_all.11 = bf16[8,4,6144]{2,1,0:T(4,128)(2,1)S(1)} all-to-all(bf16[8,4,6144]{2,1,0:T(4,128)(2,1)S(1)} %copy.39), channel_id=1, replica_groups=mesh['expert'=8,'shard'=32] {'expert'}, dimensions={0} | all-to-all | bytes 786432 | tf_op jit(solution)/shard_map/all_to_all | solution.py:81
  322.3 1.0 fusion
  (4 shorter events, 0.0 us)
Async XLA Ops:
  6.5 149.8 %copy-start = (bf16[1,256,6144]{2,1,0:T(8,128)(2,1)S(1)}, bf16[1,256,6144]{2,1,0:T(8,128)(2,1)}, u32[]{:S(2)}) copy-start(bf16[1,256,6144]{2,1,0:T(8,128)(2,1)} %param.15) | copy-start | bytes 9437188
  6.5 114.3 %all-gather.3.cloned.1.call-start = ((), (), s32[]{:S(2)}) async-start(), calls=%async_computation.4 | async-start | bytes 12976128 | tf_op jit(solution)/shard_map/all_gather | solution.py:17
  26.5 283.8 %reduce-scatter.2.cloned.1.call-start = ((), (), s32[]{:S(2)}) async-start(), calls=%async_computation.3 | async-start | bytes 12976128 | tf_op jit(solution)/shard_map/reduce_scatter | solution.py:77
  140.1 9.1 %copy-start.1 = (bf16[32,32,6144]{2,1,0:T(8,128)(2,1)S(1)}, bf16[32,32,6144]{2,1,0:T(8,128)(2,1)}, u32[]{:S(2)}) copy-start(bf16[32,32,6144]{2,1,0:T(8,128)(2,1)} %reshape.67) | copy-start | bytes 37748740
  140.1 10.0 %copy-start.2 = (bf16[1,6144,256]{2,1,0:T(8,128)(2,1)S(1)}, bf16[1,6144,256]{2,1,0:T(8,128)(2,1)}, u32[]{:S(2)}) copy-start(bf16[1,6144,256]{2,1,0:T(8,128)(2,1)} %param.14) | copy-start | bytes 9437188
Sparse Core Ops, SparseCore 0:
  26.6 94.1 all-gather.2
  163.8 146.4 reduce-scatter.1
where the time goes:
time: 333 us; the launch traced here: 330 us
  waiting for transfers between devices  241 us (72%)
  local copies, waits for them, and re-layouts  25.3 us (8%)
  blocking collectives  24.4 us (7%)
  matrix products  21.4 us (6%)
  between operations  13.5 us (4%)
  other arithmetic  4.63 us (1%)
    reduce_scatter x1, waiting for transfers between devices, on_device(): lax.psum_scatter(partial_value.astype(jnp.bfloat16), 'shard', scatter_dim...  147 us
    all_gather x1, waiting for transfers between devices, on_gathered_pieces(): parts = [lax.all_gather(slab, axis) for slab in pieces]  94.3 us
    reshape x1, local copies, waits for them, and re-layouts, expert_apply(): flat_rows = slot_rows.reshape(-1, row_shape[-1])  19.3 us
    all_to_all x1, blocking collectives, on_device(): lax.all_to_all(buffers, 'expert', split_axis=0, concat_axis=0, tiled=True)  13.7 us
    all_to_all x1, blocking collectives, on_device(): lax.all_to_all(outputs, 'expert', split_axis=0, concat_axis=0, tiled=True)  10.7 us
    dot_general x1, matrix products, expert_apply(): gate_val = jnp.dot(flat_rows, gate_proj, preferred_element_type=jnp.float32)  7.53 us
    dot_general x1, matrix products, expert_apply(): partial_out = jnp.dot(hidden, down_proj, preferred_element_type=jnp.float32)  7.39 us
  transfers between devices with their start and end apart: 2, of which 2 were waited for; matrix products, arithmetic and copies ran while one was open for 0% of the time, Pallas kernels for 0%

commit v1 on v0

v1 whole, which is shorter than its diff:
```python
import jax
import jax.numpy as jnp
from jax import lax
from jax.experimental import pallas as pl
from jax.experimental.pallas import tpu as pltpu
from jax.sharding import PartitionSpec as P

MESH = pl.DeviceIdType.MESH
F32, BF16 = jnp.float32, jnp.bfloat16

D = 6144
HALF = D // 2
FW = 256
META = 128
CHUNKS = 4


def device_of(x, y, z, core):
    return (lax.rem(z, 2) * 4 + y, (z // 2) * 8 + x * 2 + core)


def remote(src, dst, send, recv, device):
    return pltpu.make_async_remote_copy(
        src_ref=src,
        dst_ref=dst,
        send_sem=send,
        recv_sem=recv,
        device_id=device,
        device_id_type=MESH,
    )


def routing_lanes(routes, gates, cap_ref):
    lane = lax.broadcasted_iota(jnp.int32, (8, META), 1)
    row = lax.broadcasted_iota(jnp.int32, (8, META), 0)
    expert, slot = lane // 4, lane % 4
    named = [routes[:, k : k + 1] == expert for k in range(2)]
    either = (named[0] | named[1]).astype(jnp.int32)
    running = either
    for shift in (1, 2, 4):
        running = running + jnp.where(row >= shift, pltpu.roll(running, shift, 0), 0)
    rank = running - either
    limit = jnp.zeros((8, META), jnp.int32)
    for e in range(8):
        limit = jnp.where(expert == e, cap_ref[e], limit)
    held = (rank == slot) & (rank < limit)
    weights = jnp.zeros((8, META), F32)
    for k in range(2):
        weights = weights + jnp.where(named[k] & held, gates[:, k : k + 1], 0.0)
    high = weights.astype(BF16).astype(F32)
    middle = (weights - high).astype(BF16).astype(F32)
    low = weights - high - middle
    return high + pltpu.roll(middle, 32, 1) + pltpu.roll(low, 64, 1)


def kernel(
    tok_ref, gain_ref, routes_ref, gates_ref, cap_ref, wg_ref, wu_ref, wd_ref, out_ref,
    pair_src, pair_dst, ztok, sbuf, xbuf, wgu, wdn, gsend, grecv, gown, hbuf,
    ybuf, r1buf, r2buf, rbuf, yret, zsend, zret, fin_src, fin_dst,
    pair_sem, z_s, z_r, y_s, y_r, x1_s, x1_r, x2_s, x2_r, w_l, w_s, w_r, g_s, g_r, h_s, h_r,
    r1_s, r1_r, r2_s, r2_r, yr_s, yr_r, zr_s, zr_r, fin_sem,
):
    me_e, me_s = lax.axis_index("expert"), lax.axis_index("shard")
    z_lo, y = me_e // 4, lax.rem(me_e, 4)
    z = (me_s // 8) * 2 + z_lo
    x = lax.rem(me_s // 2, 4)
    core = lax.rem(me_s, 2)
    sibling = device_of(x, y, z, 1 - core)
    left = device_of(lax.rem(x + 3, 4), y, z, core)
    right = device_of(lax.rem(x + 1, 4), y, z, core)

    def at_y(r):
        return device_of(x, lax.rem(y + r, 4), z, core)

    def at_z(d):
        return device_of(x, y, lax.rem(z + d, 8), core)

    place = {0: 0, 1: 1, 7: 2, 2: 3, 6: 4, 3: 5, 5: 6, 4: 7}

    mine = pl.ds(pl.multiple_of(core * HALF, HALF), HALF)
    other = pl.ds(pl.multiple_of((1 - core) * HALF, HALF), HALF)
    local_weights = [
        pltpu.make_async_copy(wg_ref.at[0, mine], wgu.at[2], w_l.at[0]),
        pltpu.make_async_copy(wu_ref.at[0, mine], wgu.at[3], w_l.at[1]),
        pltpu.make_async_copy(wd_ref.at[0, :, mine], wdn.at[0], w_l.at[2]),
    ]
    pair_weights = [
        remote(wg_ref.at[0, other], wgu.at[0], w_s.at[0], w_r.at[0], sibling),
        remote(wu_ref.at[0, other], wgu.at[1], w_s.at[1], w_r.at[1], sibling),
        remote(wd_ref.at[0, :, other], wdn.at[1], w_s.at[2], w_r.at[2], sibling),
    ]
    for copy in local_weights:
        copy.start()

    barrier = pltpu.get_barrier_semaphore()
    greeted = [sibling, left, right] + [at_y(r) for r in (1, 2, 3)] + [at_z(d) for d in range(1, 8)]
    for device in greeted:
        pl.semaphore_signal(barrier, inc=1, device_id=device, device_id_type=MESH)

    tokens = tok_ref[...].astype(F32)
    scale = lax.rsqrt(jnp.mean(tokens * tokens, axis=-1, keepdims=True) + 1e-05)
    normed = tokens * scale * gain_ref[...]
    lanes = routing_lanes(routes_ref[...], gates_ref[...], cap_ref)
    first = core == 0
    own_half = jnp.where(first, normed[:, :HALF], normed[:, HALF:])
    pair_src[:, :HALF] = jnp.where(first, normed[:, HALF:], normed[:, :HALF]).astype(BF16)
    pair_src[:, HALF:] = lanes.astype(BF16)

    pl.semaphore_wait(barrier, len(greeted))
    pair = remote(pair_src, pair_dst, pair_sem.at[0], pair_sem.at[1], sibling)
    pair.start()
    for copy in pair_weights:
        copy.start()
    pair.wait_recv()
    their_half = pair_dst[:, :HALF].astype(F32)
    their_lanes = pair_dst[:, HALF:].astype(F32)
    ztok[0, :, :HALF] = jnp.concatenate(
        [jnp.where(first, own_half, their_half), jnp.where(first, their_half, own_half)], axis=0
    ).astype(BF16)
    ztok[0, :, HALF:] = jnp.concatenate(
        [jnp.where(first, lanes, their_lanes), jnp.where(first, their_lanes, lanes)], axis=0
    ).astype(BF16)

    def z_copy(d):
        n = place[d]
        return remote(ztok.at[0], ztok.at[n], z_s.at[n], z_r.at[n], at_z(8 - d))

    for d in (1, 7, 2, 6, 3, 5, 4):
        z_copy(d).start()

    def z_arrival(n):
        return remote(ztok.at[0], ztok.at[n], z_s.at[n], z_r.at[n], at_z(1))

    def weights_of(k, turned):
        meta = ztok[pl.ds(2 * k, 2), :, HALF:].reshape(32, META)
        shape = (64, META) if turned else (META, 64)
        lane = lax.broadcasted_iota(jnp.int32, shape, 1 if turned else 0)
        column = lax.broadcasted_iota(jnp.int32, shape, 0 if turned else 1)
        expert = z_lo * 4 + (y + column // 16) % 4
        wanted = expert * 4 + column % 4
        pick = ((lane % 32 == wanted) & (lane < 96)).astype(F32).astype(BF16)
        if turned:
            raw = lax.dot_general(pick, meta, (((1,), (1,)), ((), ())), preferred_element_type=F32)
        else:
            raw = jnp.dot(meta, pick, preferred_element_type=F32)
        shape = (64, 32) if turned else (32, 64)
        column = lax.broadcasted_iota(jnp.int32, shape, 0 if turned else 1)
        row = lax.broadcasted_iota(jnp.int32, shape, 1 if turned else 0)
        return jnp.where(row // 8 == (column // 4) % 4, raw, 0.0)

    def y_copy(k, r):
        return remote(sbuf.at[k, r - 1], xbuf.at[k, 0, 4 - r], y_s.at[k, r - 1], y_r.at[k, 3 - r], at_y(r))

    def y_arrival(k, i):
        return remote(sbuf.at[k, 0], xbuf.at[k, 0, i], y_s.at[k, 0], y_r.at[k, i - 1], at_y(1))

    def dispatch(k):
        @pl.when(k > 0)
        def _():
            z_arrival(2 * k).wait_recv()

        z_arrival(2 * k + 1).wait_recv()
        picker = jnp.where(weights_of(k, True) != 0.0, 1.0, 0.0).astype(BF16)
        step = HALF // 4
        for n in range(4):
            columns = slice(n * step, (n + 1) * step)
            slab = ztok[pl.ds(2 * k, 2), :, columns].reshape(32, step)
            slots = jnp.dot(picker, slab, preferred_element_type=F32).astype(BF16).reshape(4, 16, step)
            xbuf[k, 0, 0, :, columns] = slots[0]
            sbuf[k, :, :, columns] = slots[1:]
        for r in (2, 1, 3):
            y_copy(k, r).start()

    def x1_copies(k):
        return (
            remote(xbuf.at[k, 0], xbuf.at[k, 1], x1_s.at[k, 0], x1_r.at[k, 0], right),
            remote(xbuf.at[k, 0], xbuf.at[k, 2], x1_s.at[k, 1], x1_r.at[k, 1], left),
        )

    def x2_copies(k):
        low, high = pl.ds(0, 2), pl.ds(2, 2)
        return (
            remote(xbuf.at[k, 1, low], xbuf.at[k, 3, low], x2_s.at[k, 0], x2_r.at[k, 0], right),
            remote(xbuf.at[k, 2, high], xbuf.at[k, 3, high], x2_s.at[k, 1], x2_r.at[k, 1], left),
        )

    def gather_near(k):
        for i in (1, 3, 2):
            y_arrival(k, i).wait_recv()
        for copy in x1_copies(k):
            copy.start()

    def gather_far(k):
        for near, far in zip(x1_copies(k), x2_copies(k)):
            near.wait_recv()
            far.start()

    def pre_activations(k):
        return remote(gsend.at[k], grecv.at[k], g_s.at[k], g_r.at[k], sibling)

    def hidden_copy(k):
        return remote(hbuf.at[k, 0], hbuf.at[k, 1], h_s.at[k], h_r.at[k], sibling)

    def r1_copies(k):
        low, high = pl.ds(0, 2), pl.ds(2, 2)
        return (
            remote(ybuf.at[k, 3, low], r1buf.at[k, 0], r1_s.at[k, 0], r1_r.at[k, 0], left),
            remote(ybuf.at[k, 3, high], r1buf.at[k, 1], r1_s.at[k, 1], r1_r.at[k, 1], right),
        )

    def r2_copies(k):
        return (
            remote(ybuf.at[k, 1], r2buf.at[k, 1], r2_s.at[k, 1], r2_r.at[k, 1], left),
            remote(ybuf.at[k, 2], r2buf.at[k, 0], r2_s.at[k, 0], r2_r.at[k, 0], right),
        )

    def expert_apply(k):
        @pl.when(k == 0)
        def _():
            for copy in local_weights:
                copy.wait()
            for copy in pair_weights:
                copy.wait_recv()

        for copy in x2_copies(k):
            copy.wait_recv()

        def project(n):
            rows = xbuf[k].reshape(256, HALF)
            return jnp.dot(rows, wgu[n], preferred_element_type=F32)

        @pl.loop(0, 2)
        def _(n):
            gsend[k, n] = project(n)

        pre_activations(k).start()

        @pl.loop(0, 2)
        def _(n):
            gown[n] = project(n + 2)

        pre_activations(k).wait_recv()
        gate = gown[0] + grecv[k, 0]
        up = gown[1] + grecv[k, 1]
        hbuf[k, 0] = (gate / (1.0 + jnp.exp(-gate)) * up).astype(BF16)
        hidden_copy(k).start()
        hidden_copy(k).wait_recv()
        step = 512

        @pl.loop(0, HALF // step)
        def _(n):
            columns = pl.ds(pl.multiple_of(n * step, step), step)
            made = jnp.dot(hbuf[k, 0], wdn[0, :, columns], preferred_element_type=F32)
            made = made + jnp.dot(hbuf[k, 1], wdn[1, :, columns], preferred_element_type=F32)
            ybuf[k, :, :, :, columns] = made.astype(BF16).reshape(4, 4, 16, step)

        for copy in r1_copies(k):
            copy.start()

    def return_near(k):
        for copy in r1_copies(k):
            copy.wait_recv()
        ybuf[k, 1, 0:2] = (ybuf[k, 1, 0:2].astype(F32) + r1buf[k, 0].astype(F32)).astype(BF16)
        ybuf[k, 2, 2:4] = (ybuf[k, 2, 2:4].astype(F32) + r1buf[k, 1].astype(F32)).astype(BF16)
        for copy in r2_copies(k):
            copy.start()

    def yr_copy(k, i):
        return remote(rbuf.at[k, i - 1], yret.at[k, 4 - i], yr_s.at[k, i - 1], yr_r.at[k, 3 - i], at_y(i))

    def yr_arrival(k, r):
        return remote(rbuf.at[k, 0], yret.at[k, r], yr_s.at[k, 0], yr_r.at[k, r - 1], at_y(1))

    def return_rows(k):
        for copy in r2_copies(k):
            copy.wait_recv()
        total = ybuf[k, 0].astype(F32) + r2buf[k, 0].astype(F32) + r2buf[k, 1].astype(F32)
        total = total.astype(BF16)
        yret[k, 0] = total[0]
        rbuf[k] = total[1:]
        for i in (2, 1, 3):
            yr_copy(k, i).start()

    def zr_copy(n, d):
        return remote(zsend.at[n], zret.at[n], zr_s.at[n], zr_r.at[n], at_z(d))

    def combine(k):
        for r in (1, 3, 2):
            yr_arrival(k, r).wait_recv()
        weights = weights_of(k, False)
        high = weights.astype(BF16)
        rest = (weights - high.astype(F32)).astype(BF16)
        step = HALF // 4
        for n in range(4):
            columns = slice(n * step, (n + 1) * step)
            rows = yret[k, :, :, columns].reshape(64, step)
            made = jnp.dot(high, rows, preferred_element_type=F32)
            made = made + jnp.dot(rest, rows, preferred_element_type=F32)
            zsend[pl.ds(2 * k, 2), :, columns] = made.astype(BF16).reshape(2, 16, step)

        @pl.when(k > 0)
        def _():
            zr_copy(2 * k, 8 - k).start()

        zr_copy(2 * k + 1, k + 1).start()

    def when(k, work):
        @pl.when((k >= 0) & (k < CHUNKS))
        def _():
            work(k)

    dispatch(0)

    def step_of(t, carry):
        when(t - 5, combine)
        when(t, gather_near)
        when(t + 1, dispatch)
        when(t - 1, gather_far)
        when(t - 4, return_rows)
        when(t - 3, return_near)
        when(t - 2, expert_apply)
        return carry

    lax.fori_loop(0, CHUNKS + 5, step_of, 0)

    total = zsend[0].astype(F32)
    for n in range(1, 8):
        zr_copy(n, 1).wait_recv()
        total = total + zret[n].astype(F32)
    total = total.astype(BF16).astype(F32)
    fin_src[...] = jnp.where(first, total[8:], total[:8]).astype(BF16)
    fin = remote(fin_src, fin_dst, fin_sem.at[0], fin_sem.at[1], sibling)
    fin.start()
    kept = jnp.where(first, total[:8], total[8:])
    fin.wait_recv()
    theirs = fin_dst[...].astype(F32)
    out_ref[:, :HALF] = jnp.where(first, kept, theirs).astype(BF16)
    out_ref[:, HALF:] = jnp.where(first, theirs, kept).astype(BF16)

    fin.wait_send()
    pair.wait_send()
    for copy in pair_weights:
        copy.wait_send()
    for d in range(1, 8):
        z_copy(d).wait_send()
        zr_copy(d, 1).wait_send()

    def sent(k, carry):
        for r in (1, 2, 3):
            y_copy(k, r).wait_send()
            yr_copy(k, r).wait_send()
        for copy in x1_copies(k) + x2_copies(k) + r1_copies(k) + r2_copies(k):
            copy.wait_send()
        pre_activations(k).wait_send()
        hidden_copy(k).wait_send()
        return carry

    lax.fori_loop(0, CHUNKS, sent, 0)


def on_device(tokens, norm_gain, routes, gate_weights, capacity, w_gate, w_up, w_down):
    vmem, smem = pl.BlockSpec(memory_space=pltpu.VMEM), pl.BlockSpec(memory_space=pltpu.SMEM)
    whole = pl.BlockSpec(memory_space=pl.ANY)
    sems = pltpu.SemaphoreType.DMA
    k = CHUNKS
    return pl.pallas_call(
        kernel,
        out_shape=jax.ShapeDtypeStruct((8, D), BF16),
        in_specs=[vmem, vmem, vmem, vmem, smem, whole, whole, whole],
        out_specs=vmem,
        scratch_shapes=[
            pltpu.VMEM((8, HALF + META), BF16),
            pltpu.VMEM((8, HALF + META), BF16),
            pltpu.VMEM((8, 16, HALF + META), BF16),
            pltpu.VMEM((k, 3, 16, HALF), BF16),
            pltpu.VMEM((k, 4, 4, 16, HALF), BF16),
            pltpu.VMEM((4, HALF, FW), BF16),
            pltpu.VMEM((2, FW, HALF), BF16),
            pltpu.VMEM((k, 2, 256, FW), F32),
            pltpu.VMEM((k, 2, 256, FW), F32),
            pltpu.VMEM((2, 256, FW), F32),
            pltpu.VMEM((k, 2, 256, FW), BF16),
            pltpu.VMEM((k, 4, 4, 16, HALF), BF16),
            pltpu.VMEM((k, 2, 2, 16, HALF), BF16),
            pltpu.VMEM((k, 2, 4, 16, HALF), BF16),
            pltpu.VMEM((k, 3, 16, HALF), BF16),
            pltpu.VMEM((k, 4, 16, HALF), BF16),
            pltpu.VMEM((8, 16, HALF), BF16),
            pltpu.VMEM((8, 16, HALF), BF16),
            pltpu.VMEM((8, HALF), BF16),
            pltpu.VMEM((8, HALF), BF16),
            sems((2,)),
            sems((8,)), sems((8,)),
            sems((k, 3)), sems((k, 3)),
            sems((k, 2)), sems((k, 2)),
            sems((k, 2)), sems((k, 2)),
            sems((3,)), sems((3,)), sems((3,)),
            sems((k,)), sems((k,)),
            sems((k,)), sems((k,)),
            sems((k, 2)), sems((k, 2)),
            sems((k, 2)), sems((k, 2)),
            sems((k, 3)), sems((k, 3)),
            sems((8,)), sems((8,)),
            sems((2,)),
        ],
        compiler_params=pltpu.CompilerParams(
            collective_id=0, has_side_effects=True, vmem_limit_bytes=67043328
        ),
    )(tokens, norm_gain[None], routes, gate_weights, capacity, w_gate, w_up, w_down)


def solution(mesh):
    in_specs = (
        P(("expert", "shard"), None),
        P(),
        P(("expert", "shard"), None),
        P(("expert", "shard"), None),
        P(),
        P("expert", None, "shard"),
        P("expert", None, "shard"),
        P("expert", "shard", None),
    )
    out_specs = P(("expert", "shard"), None)
    return jax.shard_map(
        on_device, mesh=mesh, in_specs=in_specs, out_specs=out_specs, check_vma=False
    )
```

time: 333 us -> 155 us (0.47)
  waiting for transfers between devices: 241 us -> 0 us
  Pallas kernels: 0 us -> 150 us
  blocking collectives: 24.4 us -> 0 us
  matrix products: 21.4 us -> 0 us
  local copies, waits for them, and re-layouts: 25.3 us -> 4.23 us
  between operations: 13.5 us -> 0.01 us
  other arithmetic: 4.63 us -> 0 us
    pallas_call x0 -> x1, Pallas kernels: none -> 150 us  [on_device(): pl.pallas_call(kernel, out_shape=jax.ShapeDtypeStruct((8, D), BF16), in_s...]
    reduce_scatter x1 -> x0, waiting for transfers between devices: 147 us -> none  [on_device(): lax.psum_scatter(partial_value.astype(jnp.bfloat16), 'shard', scatter_dim...]
    all_gather x1 -> x0, waiting for transfers between devices: 94.3 us -> none  [on_gathered_pieces(): parts = [lax.all_gather(slab, axis) for slab in pieces]]
    all_to_all x2 -> x0, blocking collectives: 24.4 us -> none  [the longest x1 13.7 us: on_device(): lax.all_to_all(buffers, 'expert', split_axis=0, concat_axis=0, tiled=True)]
    dot_general x5 -> x0, matrix products: 21.4 us -> none  [the longest x1 7.53 us: expert_apply(): gate_val = jnp.dot(flat_rows, gate_proj, preferred_element_type=jnp.float32)]
    reshape x1 -> x0, local copies, waits for them, and re-layouts: 19.3 us -> none  [expert_apply(): flat_rows = slot_rows.reshape(-1, row_shape[-1])]
  transfers between devices with their start and end apart: 2 -> 0, of which waited for: 2 -> 0; matrix products, arithmetic and copies ran while one was open for 0% -> 0% of each run, Pallas kernels for 0% -> 0%
where the time goes in v1:
time: 155 us
  Pallas kernels  150 us (97%)
  local copies, waits for them, and re-layouts  4.23 us (3%)
    pallas_call x1, Pallas kernels, on_device(): pl.pallas_call(kernel, out_shape=jax.ShapeDtypeStruct((8, D), BF16), in_s...  150 us
    unnamed x3, local copies, waits for them, and re-layouts  4.23 us

profile of v1, /device:TPU:1, one launch (start us, length us, event | category | flops | bytes accessed | tf_op | source)
XLA Modules:
  0.0 154.5 jit_solution(793409580385676488)
XLA Ops:
  0.0 1.3 copy.9.routes_ref
  1.3 1.3 copy.10.gates_ref
  2.7 150.3 %shard_map.82 = bf16[8,6144]{1,0:T(8,128)(2,1)} custom-call(bf16[8,6144]{1,0:T(8,128)(2,1)} %tok_ref.1, f32[1,6144]{1,0:T(1,128)} %bitcast.1, s32[8,2]{1,0:T(8,128)} %copy.9.routes_ref, f32[8,2]{1,0:T(8,128)} %copy.10.gates_ref, s32[8]{0:T(128)} %cap_ref.1, bf16[1,6144,256]{2,1,0:T(8,128)(2,1)} %wg_ref.1, bf16[1,6144,256]{2,1,0:T(8,128)(2,1)} %wu_ref.1, ...), custom_call_target="tpu_custom_call" | custom-call | tf_op jit(solution)/shard_map/pallas_call | solution.py:366
  153.0 1.5 copy.12

commit v2 on v1

v2 whole, which is shorter than its diff:
```python
import jax
import jax.numpy as jnp
from jax import lax
from jax.experimental import pallas as pl
from jax.experimental.pallas import tpu as pltpu
from jax.sharding import PartitionSpec as P

MESH = pl.DeviceIdType.MESH
F32, BF16 = jnp.float32, jnp.bfloat16

D = 6144
HALF = D // 2
FW = 256
META = 128
CHUNKS = 4
A = 1792
B = HALF - A
TILE = 256


def device_of(x, y, z, core):
    return (lax.rem(z, 2) * 4 + y, (z // 2) * 8 + x * 2 + core)


def remote(src, dst, send, recv, device):
    return pltpu.make_async_remote_copy(
        src_ref=src,
        dst_ref=dst,
        send_sem=send,
        recv_sem=recv,
        device_id=device,
        device_id_type=MESH,
    )


def columns_of(pair):
    row = lax.broadcasted_iota(jnp.int32, (8, 8), 0)
    lane = lax.broadcasted_iota(jnp.int32, (8, 8), 1)
    spread = [jnp.broadcast_to(pair[k : k + 1, :], (8, 8)) for k in range(2)]
    zero = jnp.zeros((8, 8), pair.dtype)
    return [jnp.sum(jnp.where(row == lane, s, zero), axis=1, keepdims=True) for s in spread]


def routing_lanes(routes, gates, cap_ref):
    lane = lax.broadcasted_iota(jnp.int32, (8, META), 1)
    row = lax.broadcasted_iota(jnp.int32, (8, META), 0)
    expert, slot = lane // 4, lane % 4
    named = [routes[k] == expert for k in range(2)]
    either = (named[0] | named[1]).astype(jnp.int32)
    running = either
    for shift in (1, 2, 4):
        running = running + jnp.where(row >= shift, pltpu.roll(running, shift, 0), 0)
    rank = running - either
    limit = jnp.zeros((8, META), jnp.int32)
    for e in range(8):
        limit = jnp.where(expert == e, cap_ref[e], limit)
    held = (rank == slot) & (rank < limit)
    weights = jnp.zeros((8, META), F32)
    for k in range(2):
        weights = weights + jnp.where(named[k] & held, gates[k], 0.0)
    high = weights.astype(BF16).astype(F32)
    middle = (weights - high).astype(BF16).astype(F32)
    low = weights - high - middle
    return high + pltpu.roll(middle, 32, 1) + pltpu.roll(low, 64, 1)


def kernel(
    tok_ref, gain_ref, routes_ref, gates_ref, cap_ref, wg_ref, wu_ref, wd_ref, out_ref,
    pair_src, pair_dst, ztok, sbuf_a, sbuf_b, xtok, xbuf_a, xbuf_b, wgu, wdn, gsend, grecv, gown, hbuf,
    ybuf_a, ybuf_b, r1buf, r2buf, rbuf, yret_a, yret_b, tokb, t1buf, t2buf, zsend, zret, fin_src, fin_dst,
    pair_sem, z_s, z_r, ya_s, ya_r, yb_s, yb_r, x1_s, x1_r, x2_s, x2_r, b1_s, b1_r, b2_s, b2_r,
    w_l, w_s, w_r, g_s, g_r, h_s, h_r, r1_s, r1_r, r2_s, r2_r, t1_s, t1_r, t2_s, t2_r,
    yra_s, yra_r, yrb_s, yrb_r, zr_s, zr_r, fin_sem,
):
    me_e, me_s = lax.axis_index("expert"), lax.axis_index("shard")
    z_lo, y = me_e // 4, lax.rem(me_e, 4)
    z = (me_s // 8) * 2 + z_lo
    x = lax.rem(me_s // 2, 4)
    core = lax.rem(me_s, 2)
    sibling = device_of(x, y, z, 1 - core)
    left = device_of(lax.rem(x + 3, 4), y, z, core)
    right = device_of(lax.rem(x + 1, 4), y, z, core)

    def at_y(r):
        return device_of(x, lax.rem(y + r, 4), z, core)

    def at_z(d):
        return device_of(x, y, lax.rem(z + d, 8), core)

    barrier = pltpu.get_barrier_semaphore()
    greeted = [at_z(d) for d in (4, 3, 5, 2, 6, 1, 7)] + [at_y(r) for r in (2, 1, 3)] + [left, right, sibling]
    for device in greeted:
        pl.semaphore_signal(barrier, inc=1, device_id=device, device_id_type=MESH)

    own = 1

    def place(d):
        return d - 1 if d % 2 else (8 - d) % 8 + 1

    mine = pl.ds(pl.multiple_of(core * HALF, HALF), HALF)
    other = pl.ds(pl.multiple_of((1 - core) * HALF, HALF), HALF)
    local_weights = [
        pltpu.make_async_copy(wg_ref.at[0, mine], wgu.at[2], w_l.at[0]),
        pltpu.make_async_copy(wu_ref.at[0, mine], wgu.at[3], w_l.at[1]),
        pltpu.make_async_copy(wd_ref.at[0, :, mine], wdn.at[0], w_l.at[2]),
    ]
    pair_weights = [
        remote(wg_ref.at[0, other], wgu.at[0], w_s.at[0], w_r.at[0], sibling),
        remote(wu_ref.at[0, other], wgu.at[1], w_s.at[1], w_r.at[1], sibling),
        remote(wd_ref.at[0, :, other], wdn.at[1], w_s.at[2], w_r.at[2], sibling),
    ]
    for copy in local_weights:
        copy.start()

    tokens = tok_ref[...].astype(F32)
    scale = lax.rsqrt(jnp.mean(tokens * tokens, axis=-1, keepdims=True) + 1e-05)
    normed = tokens * scale * gain_ref[...]
    lanes = routing_lanes(columns_of(routes_ref[...]), columns_of(gates_ref[...]), cap_ref)
    first = core == 0
    own_half = jnp.where(first, normed[:, :HALF], normed[:, HALF:])
    pair_src[:, :HALF] = jnp.where(first, normed[:, HALF:], normed[:, :HALF]).astype(BF16)
    pair_src[:, HALF:] = lanes.astype(BF16)

    pl.semaphore_wait(barrier, len(greeted))
    pair = remote(pair_src, pair_dst, pair_sem.at[0], pair_sem.at[1], sibling)
    pair.start()
    for copy in pair_weights:
        copy.start()
    pair.wait_recv()
    their_half = pair_dst[:, :HALF].astype(F32)
    their_lanes = pair_dst[:, HALF:].astype(F32)
    ztok[own, :, :HALF] = jnp.concatenate(
        [jnp.where(first, own_half, their_half), jnp.where(first, their_half, own_half)], axis=0
    ).astype(BF16)
    ztok[own, :, HALF:] = jnp.concatenate(
        [jnp.where(first, lanes, their_lanes), jnp.where(first, their_lanes, lanes)], axis=0
    ).astype(BF16)

    def z_copy(d):
        n = place(d)
        return remote(ztok.at[own], ztok.at[n], z_s.at[n], z_r.at[n], at_z(8 - d))

    for d in (1, 3, 6, 5, 4, 7, 2):
        z_copy(d).start()

    def z_arrival(n):
        return remote(ztok.at[own], ztok.at[n], z_s.at[n], z_r.at[n], at_z(1))

    def weights_of(meta, turned):
        shape = (64, META) if turned else (META, 64)
        lane = lax.broadcasted_iota(jnp.int32, shape, 1 if turned else 0)
        column = lax.broadcasted_iota(jnp.int32, shape, 0 if turned else 1)
        expert = z_lo * 4 + (y + column // 16) % 4
        wanted = expert * 4 + column % 4
        pick = ((lane % 32 == wanted) & (lane < 96)).astype(F32).astype(BF16)
        if turned:
            raw = lax.dot_general(pick, meta, (((1,), (1,)), ((), ())), preferred_element_type=F32)
        else:
            raw = jnp.dot(meta, pick, preferred_element_type=F32)
        shape = (64, 32) if turned else (32, 64)
        column = lax.broadcasted_iota(jnp.int32, shape, 0 if turned else 1)
        row = lax.broadcasted_iota(jnp.int32, shape, 1 if turned else 0)
        return jnp.where(row // 8 == (column // 4) % 4, raw, 0.0)

    def picker_of(meta):
        return jnp.where(weights_of(meta, True) != 0.0, 1.0, 0.0).astype(BF16)

    def picked(picker, slab):
        return jnp.dot(picker, slab, preferred_element_type=F32).astype(BF16).reshape(4, 16, slab.shape[1])

    def combined(weights, rows):
        high = weights.astype(BF16)
        rest = (weights - high.astype(F32)).astype(BF16)
        made = jnp.dot(high, rows, preferred_element_type=F32) + jnp.dot(rest, rows, preferred_element_type=F32)
        return made.astype(BF16).reshape(2, 16, rows.shape[1])

    def ya_copy(k, r):
        return remote(sbuf_a.at[k, r - 1], xbuf_a.at[k, 0, 4 - r], ya_s.at[k, r - 1], ya_r.at[k, 3 - r], at_y(r))

    PARTS = ((0, 1), (1, 2), (3, 1))

    def yb_copy(k, part, r):
        rows = pl.ds(*PARTS[part])
        return remote(
            sbuf_b.at[k, r - 1, rows], xbuf_b.at[k, rows, 4 - r], yb_s.at[k, part, r - 1], yb_r.at[k, part, 3 - r], at_y(r)
        )

    def x1_copies(k):
        return (
            remote(xbuf_a.at[k, 0], xbuf_a.at[k, 1], x1_s.at[k, 0], x1_r.at[k, 0], right),
            remote(xbuf_a.at[k, 0], xbuf_a.at[k, 2], x1_s.at[k, 1], x1_r.at[k, 1], left),
        )

    def x2_copies(k):
        low, high = pl.ds(0, 2), pl.ds(2, 2)
        return (
            remote(xbuf_a.at[k, 1, low], xbuf_a.at[k, 3, low], x2_s.at[k, 0], x2_r.at[k, 0], right),
            remote(xbuf_a.at[k, 2, high], xbuf_a.at[k, 3, high], x2_s.at[k, 1], x2_r.at[k, 1], left),
        )

    def b1_copies(k):
        source = ztok.at[pl.ds(2 * k, 2), :, A:]
        return (
            remote(source, xtok.at[k, 0], b1_s.at[k, 0], b1_r.at[k, 0], right),
            remote(source, xtok.at[k, 1], b1_s.at[k, 1], b1_r.at[k, 1], left),
        )

    def b2_copies(k):
        return (
            remote(xtok.at[k, 0, 0], xtok.at[k, 2, 0], b2_s.at[k, 0], b2_r.at[k, 0], right),
            remote(xtok.at[k, 1, 1], xtok.at[k, 2, 1], b2_s.at[k, 1], b2_r.at[k, 1], left),
        )

    def dispatch(k):
        z_arrival(2 * k).wait_recv()

        @pl.when(k > 0)
        def _():
            z_arrival(2 * k + 1).wait_recv()

        for copy in b1_copies(k):
            copy.start()
        picker = picker_of(ztok[pl.ds(2 * k, 2), :, HALF:].reshape(32, META))

        def slots_at(start):
            return picked(picker, ztok[pl.ds(2 * k, 2), :, start : start + TILE].reshape(32, TILE))

        for start in range(0, A, TILE):
            slots = slots_at(start)
            xbuf_a[k, 0, 0, :, start : start + TILE] = slots[0]
            sbuf_a[k, :, :, start : start + TILE] = slots[1:]
        for r in (2, 1, 3):
            ya_copy(k, r).start()
        for start in range(0, B, TILE):
            slots = slots_at(A + start)
            xbuf_b[k, 0, 0, :, start : start + TILE] = slots[0]
            sbuf_b[k, :, 0, :, start : start + TILE] = slots[1:]
        for r in (2, 1, 3):
            yb_copy(k, 0, r).start()

    def dispatch_from(k, rel):
        picker = picker_of(xtok[k, rel - 1, :, :, B:].reshape(32, META))
        for start in range(0, B, TILE):
            slots = picked(picker, xtok[k, rel - 1, :, :, start : start + TILE].reshape(32, TILE))
            xbuf_b[k, rel, 0, :, start : start + TILE] = slots[0]
            sbuf_b[k, :, rel, :, start : start + TILE] = slots[1:]

    def gather_near(k):
        for near, far in zip(b1_copies(k), b2_copies(k)):
            near.wait_recv()
            far.start()
        for r in (1, 3, 2):
            ya_copy(k, r).wait_recv()
        for copy in x1_copies(k):
            copy.start()

        @pl.loop(1, 3)
        def _(rel):
            dispatch_from(k, rel)

        for r in (2, 1, 3):
            yb_copy(k, 1, r).start()

    def gather_far(k):
        for copy in b2_copies(k):
            copy.wait_recv()
        dispatch_from(k, 3)
        for r in (2, 1, 3):
            yb_copy(k, 2, r).start()
        for near, far in zip(x1_copies(k), x2_copies(k)):
            near.wait_recv()
            far.start()

    def pre_activations(k):
        return remote(gsend.at[k], grecv.at[k], g_s.at[k], g_r.at[k], sibling)

    def hidden_copy(k):
        return remote(hbuf.at[k, 0], hbuf.at[k, 1], h_s.at[k], h_r.at[k], sibling)

    def r1_copies(k):
        low, high = pl.ds(0, 2), pl.ds(2, 2)
        return (
            remote(ybuf_a.at[k, 3, low], r1buf.at[k, 0], r1_s.at[k, 0], r1_r.at[k, 0], left),
            remote(ybuf_a.at[k, 3, high], r1buf.at[k, 1], r1_s.at[k, 1], r1_r.at[k, 1], right),
        )

    def r2_copies(k):
        return (
            remote(ybuf_a.at[k, 1], r2buf.at[k, 1], r2_s.at[k, 1], r2_r.at[k, 1], left),
            remote(ybuf_a.at[k, 2], r2buf.at[k, 0], r2_s.at[k, 0], r2_r.at[k, 0], right),
        )

    def yra_copy(k, i):
        return remote(rbuf.at[k, i - 1], yret_a.at[k, 4 - i], yra_s.at[k, i - 1], yra_r.at[k, 3 - i], at_y(i))

    def yrb_copy(k, i):
        return remote(ybuf_b.at[k, :, i], yret_b.at[k, :, 3 - i], yrb_s.at[k, i - 1], yrb_r.at[k, 3 - i], at_y(i))

    def t1_copies(k):
        return (
            remote(tokb.at[k, 3, 0], t1buf.at[k, 0], t1_s.at[k, 0], t1_r.at[k, 0], left),
            remote(tokb.at[k, 3, 1], t1buf.at[k, 1], t1_s.at[k, 1], t1_r.at[k, 1], right),
        )

    def t2_copies(k):
        return (
            remote(tokb.at[k, 1], t2buf.at[k, 1], t2_s.at[k, 1], t2_r.at[k, 1], left),
            remote(tokb.at[k, 2], t2buf.at[k, 0], t2_s.at[k, 0], t2_r.at[k, 0], right),
        )

    def expert_apply(k):
        @pl.when(k == 0)
        def _():
            for copy in local_weights:
                copy.wait()
            for copy in pair_weights:
                copy.wait_recv()

        for copy in x2_copies(k):
            copy.wait_recv()
        for part in range(3):
            for r in (1, 3, 2):
                yb_copy(k, part, r).wait_recv()

        def project(n):
            made = jnp.dot(xbuf_a[k].reshape(256, A), wgu[n, :A], preferred_element_type=F32)
            return made + jnp.dot(xbuf_b[k].reshape(256, B), wgu[n, A:], preferred_element_type=F32)

        @pl.loop(0, 2)
        def _(n):
            gsend[k, n] = project(n)

        pre_activations(k).start()

        @pl.loop(0, 2)
        def _(n):
            gown[n] = project(n + 2)

        pre_activations(k).wait_recv()
        gate = gown[0] + grecv[k, 0]
        up = gown[1] + grecv[k, 1]
        hbuf[k, 0] = (gate / (1.0 + jnp.exp(-gate)) * up).astype(BF16)
        hidden_copy(k).start()
        hidden_copy(k).wait_recv()

        def outputs(columns):
            made = jnp.dot(hbuf[k, 0], wdn[0, :, columns], preferred_element_type=F32)
            made = made + jnp.dot(hbuf[k, 1], wdn[1, :, columns], preferred_element_type=F32)
            return made.astype(BF16).reshape(4, 4, 16, TILE)

        @pl.loop(0, B // TILE)
        def _(n):
            start = pl.multiple_of(n * TILE, TILE)
            ybuf_b[k, :, :, :, pl.ds(start, TILE)] = outputs(pl.ds(pl.multiple_of(A + start, TILE), TILE))

        for i in (2, 1, 3):
            yrb_copy(k, i).start()

        @pl.loop(0, A // TILE)
        def _(n):
            start = pl.multiple_of(n * TILE, TILE)
            ybuf_a[k, :, :, :, pl.ds(start, TILE)] = outputs(pl.ds(start, TILE))

        for copy in r1_copies(k):
            copy.start()

    def plus(ref, *others):
        total = ref[...].astype(F32)
        for term in others:
            total = total + term[...].astype(F32)
        return total.astype(BF16)

    def return_near(k):
        for copy in r1_copies(k):
            copy.wait_recv()
        ybuf_a[k, 1, 0:2] = plus(ybuf_a.at[k, 1, 0:2], r1buf.at[k, 0])
        ybuf_a[k, 2, 2:4] = plus(ybuf_a.at[k, 2, 2:4], r1buf.at[k, 1])
        for copy in r2_copies(k):
            copy.start()
        for i in (1, 3, 2):
            yrb_copy(k, i).wait_recv()

        def combine_for(rel, meta):
            weights = weights_of(meta.reshape(32, META), False)
            for start in range(0, B, TILE):
                columns = slice(start, start + TILE)
                rows = jnp.concatenate([ybuf_b[k, rel, 0, :, columns][None], yret_b[k, rel, :, :, columns]], axis=0)
                tokb[k, rel, :, :, columns] = combined(weights, rows.reshape(64, TILE))

        combine_for(3, xtok[k, 2, :, :, B:])
        for copy in t1_copies(k):
            copy.start()
        combine_for(0, ztok[pl.ds(2 * k, 2), :, HALF:])

        @pl.loop(1, 3)
        def _(rel):
            combine_for(rel, xtok[k, rel - 1, :, :, B:])

    def return_rows(k):
        for copy in t1_copies(k):
            copy.wait_recv()
        tokb[k, 1, 0] = plus(tokb.at[k, 1, 0], t1buf.at[k, 0])
        tokb[k, 2, 1] = plus(tokb.at[k, 2, 1], t1buf.at[k, 1])
        for copy in t2_copies(k):
            copy.start()
        for copy in r2_copies(k):
            copy.wait_recv()
        total = plus(ybuf_a.at[k, 0], r2buf.at[k, 0], r2buf.at[k, 1])
        yret_a[k, 0] = total[0]
        rbuf[k] = total[1:]
        for i in (2, 1, 3):
            yra_copy(k, i).start()

    def zr_copy(n, d):
        return remote(zsend.at[n], zret.at[n], zr_s.at[n], zr_r.at[n], at_z(d))

    def combine(k):
        for copy in t2_copies(k):
            copy.wait_recv()
        zsend[pl.ds(2 * k, 2), :, A:] = plus(tokb.at[k, 0], t2buf.at[k, 0], t2buf.at[k, 1])
        for r in (1, 3, 2):
            yra_copy(k, r).wait_recv()
        weights = weights_of(ztok[pl.ds(2 * k, 2), :, HALF:].reshape(32, META), False)
        for start in range(0, A, TILE):
            columns = slice(start, start + TILE)
            zsend[pl.ds(2 * k, 2), :, columns] = combined(weights, yret_a[k, :, :, columns].reshape(64, TILE))
        zr_copy(2 * k, 2 * k + 1).start()

        @pl.when(k > 0)
        def _():
            zr_copy(2 * k + 1, 8 - 2 * k).start()

    def when(k, work):
        @pl.when((k >= 0) & (k < CHUNKS))
        def _():
            work(k)

    dispatch(0)

    def step_of(t, carry):
        when(t - 5, combine)
        when(t, gather_near)
        when(t + 1, dispatch)
        when(t - 1, gather_far)
        when(t - 4, return_rows)
        when(t - 3, return_near)
        when(t - 2, expert_apply)
        return carry

    lax.fori_loop(0, CHUNKS + 5, step_of, 0)

    total = zsend[own].astype(F32)
    for n in (0, 2, 3, 4, 5, 6, 7):
        zr_copy(n, 1).wait_recv()
        total = total + zret[n].astype(F32)
    total = total.astype(BF16).astype(F32)
    fin_src[...] = jnp.where(first, total[8:], total[:8]).astype(BF16)
    fin = remote(fin_src, fin_dst, fin_sem.at[0], fin_sem.at[1], sibling)
    fin.start()
    kept = jnp.where(first, total[:8], total[8:])
    fin.wait_recv()
    theirs = fin_dst[...].astype(F32)
    out_ref[:, :HALF] = jnp.where(first, kept, theirs).astype(BF16)
    out_ref[:, HALF:] = jnp.where(first, theirs, kept).astype(BF16)

    fin.wait_send()
    pair.wait_send()
    for copy in pair_weights:
        copy.wait_send()
    for d in range(1, 8):
        z_copy(d).wait_send()
    for n in (0, 2, 3, 4, 5, 6, 7):
        zr_copy(n, 1).wait_send()

    def sent(k, carry):
        for r in (1, 2, 3):
            ya_copy(k, r).wait_send()
            yra_copy(k, r).wait_send()
            yrb_copy(k, r).wait_send()
            for part in range(3):
                yb_copy(k, part, r).wait_send()
        for copies in (x1_copies, x2_copies, b1_copies, b2_copies, r1_copies, r2_copies, t1_copies, t2_copies):
            for copy in copies(k):
                copy.wait_send()
        pre_activations(k).wait_send()
        hidden_copy(k).wait_send()
        return carry

    lax.fori_loop(0, CHUNKS, sent, 0)


def on_device(tokens, norm_gain, routes, gate_weights, capacity, w_gate, w_up, w_down):
    vmem, smem = pl.BlockSpec(memory_space=pltpu.VMEM), pl.BlockSpec(memory_space=pltpu.SMEM)
    whole = pl.BlockSpec(memory_space=pl.ANY)
    k = CHUNKS

    def held(*shape, dtype=BF16):
        return pltpu.VMEM(shape, dtype)

    def sems(*shape):
        return [pltpu.SemaphoreType.DMA(shape)]

    return pl.pallas_call(
        kernel,
        out_shape=jax.ShapeDtypeStruct((8, D), BF16),
        in_specs=[vmem, vmem, vmem, vmem, smem, whole, whole, whole],
        out_specs=vmem,
        scratch_shapes=[
            held(8, HALF + META),
            held(8, HALF + META),
            held(8, 16, HALF + META),
            held(k, 3, 16, A),
            held(k, 3, 4, 16, B),
            held(k, 3, 2, 16, B + META),
            held(k, 4, 4, 16, A),
            held(k, 4, 4, 16, B),
            held(4, HALF, FW),
            held(2, FW, HALF),
            held(k, 2, 256, FW, dtype=F32),
            held(k, 2, 256, FW, dtype=F32),
            held(2, 256, FW, dtype=F32),
            held(k, 2, 256, FW),
            held(k, 4, 4, 16, A),
            held(k, 4, 4, 16, B),
            held(k, 2, 2, 16, A),
            held(k, 2, 4, 16, A),
            held(k, 3, 16, A),
            held(k, 4, 16, A),
            held(k, 4, 3, 16, B),
            held(k, 4, 2, 16, B),
            held(k, 2, 16, B),
            held(k, 2, 2, 16, B),
            held(8, 16, HALF),
            held(8, 16, HALF),
            held(8, HALF),
            held(8, HALF),
        ]
        + sems(2)
        + sems(8) * 2
        + sems(k, 3) * 2
        + sems(k, 3, 3) * 2
        + sems(k, 2) * 8
        + sems(3) * 3
        + sems(k) * 4
        + sems(k, 2) * 8
        + sems(k, 3) * 4
        + sems(8) * 2
        + sems(2),
        compiler_params=pltpu.CompilerParams(
            collective_id=0, has_side_effects=True, vmem_limit_bytes=67043328
        ),
    )(tokens, norm_gain[None], routes.T, gate_weights.T, capacity, w_gate, w_up, w_down)


def solution(mesh):
    in_specs = (
        P(("expert", "shard"), None),
        P(),
        P(("expert", "shard"), None),
        P(("expert", "shard"), None),
        P(),
        P("expert", None, "shard"),
        P("expert", None, "shard"),
        P("expert", "shard", None),
    )
    out_specs = P(("expert", "shard"), None)
    return jax.shard_map(
        on_device, mesh=mesh, in_specs=in_specs, out_specs=out_specs, check_vma=False
    )
```

time: 155 us -> 134 us (0.86)
  Pallas kernels: 150 us -> 132 us
  local copies, waits for them, and re-layouts: 4.23 us -> 1.54 us
    pallas_call x1, Pallas kernels: 150 us -> 132 us  [on_device(): pl.pallas_call(kernel, out_shape=jax.ShapeDtypeStruct((8, D), BF16), in_s...]
    unnamed x3 -> x1, local copies, waits for them, and re-layouts: 4.23 us -> 1.54 us
where the time goes in v2:
time: 134 us
  Pallas kernels  132 us (99%)
  local copies, waits for them, and re-layouts  1.54 us (1%)
    pallas_call x1, Pallas kernels, on_device(): pl.pallas_call(kernel, out_shape=jax.ShapeDtypeStruct((8, D), BF16), in_s...  132 us

profile of v2, /device:TPU:1, one launch (start us, length us, event | category | flops | bytes accessed | tf_op | source)
XLA Modules:
  0.0 133.7 jit_solution(6087236679613111678)
XLA Ops:
  0.0 132.2 %shard_map.82 = bf16[8,6144]{1,0:T(8,128)(2,1)} custom-call(bf16[8,6144]{1,0:T(8,128)(2,1)} %tok_ref.1, f32[1,6144]{1,0:T(1,128)} %bitcast.3, s32[2,8]{1,0:T(2,128)} %bitcast.4, f32[2,8]{1,0:T(2,128)} %bitcast.5, s32[8]{0:T(128)} %cap_ref.1, bf16[1,6144,256]{2,1,0:T(8,128)(2,1)} %wg_ref.1, bf16[1,6144,256]{2,1,0:T(8,128)(2,1)} %wu_ref.1, ...), custom_call_target="tpu_custom_call" | custom-call | tf_op jit(solution)/shard_map/pallas_call | solution.py:503
  132.2 1.5 %copy.10 = bf16[8,6144]{1,0:T(8,128)(2,1)} copy(bf16[8,6144]{1,0:T(8,128)(2,1)} %shard_map.82) | data formatting | bytes 196608

commit v3 on v2

--- a/solution.py
+++ b/solution.py
@@ -93,9 +93,13 @@
         pl.semaphore_signal(barrier, inc=1, device_id=device, device_id_type=MESH)
 
     own = 1
+    TURNS = (0, 2, 4, 6)
+
+    def turn(k):
+        return 2 * k
 
     def place(d):
-        return d - 1 if d % 2 else (8 - d) % 8 + 1
+        return 2 * TURNS.index(d - 1) if d % 2 else 2 * TURNS.index((8 - d) % 8) + 1
 
     mine = pl.ds(pl.multiple_of(core * HALF, HALF), HALF)
     other = pl.ds(pl.multiple_of((1 - core) * HALF, HALF), HALF)
@@ -308,7 +312,7 @@
             remote(tokb.at[k, 2], t2buf.at[k, 0], t2_s.at[k, 0], t2_r.at[k, 0], right),
         )
 
-    def expert_apply(k):
+    def expert_hidden(k):
         @pl.when(k == 0)
         def _():
             for copy in local_weights:
@@ -341,6 +345,8 @@
         up = gown[1] + grecv[k, 1]
         hbuf[k, 0] = (gate / (1.0 + jnp.exp(-gate)) * up).astype(BF16)
         hidden_copy(k).start()
+
+    def expert_out(k):
         hidden_copy(k).wait_recv()
 
         def outputs(columns):
@@ -348,18 +354,14 @@
             made = made + jnp.dot(hbuf[k, 1], wdn[1, :, columns], preferred_element_type=F32)
             return made.astype(BF16).reshape(4, 4, 16, TILE)
 
-        @pl.loop(0, B // TILE)
-        def _(n):
-            start = pl.multiple_of(n * TILE, TILE)
-            ybuf_b[k, :, :, :, pl.ds(start, TILE)] = outputs(pl.ds(pl.multiple_of(A + start, TILE), TILE))
+        for start in range(0, B, TILE):
+            ybuf_b[k, :, :, :, start : start + TILE] = outputs(slice(A + start, A + start + TILE))
 
         for i in (2, 1, 3):
             yrb_copy(k, i).start()
 
-        @pl.loop(0, A // TILE)
-        def _(n):
-            start = pl.multiple_of(n * TILE, TILE)
-            ybuf_a[k, :, :, :, pl.ds(start, TILE)] = outputs(pl.ds(start, TILE))
+        for start in range(0, A, TILE):
+            ybuf_a[k, :, :, :, start : start + TILE] = outputs(slice(start, start + TILE))
 
         for copy in r1_copies(k):
             copy.start()
@@ -424,11 +426,11 @@
         for start in range(0, A, TILE):
             columns = slice(start, start + TILE)
             zsend[pl.ds(2 * k, 2), :, columns] = combined(weights, yret_a[k, :, :, columns].reshape(64, TILE))
-        zr_copy(2 * k, 2 * k + 1).start()
+        zr_copy(2 * k, turn(k) + 1).start()
 
         @pl.when(k > 0)
         def _():
-            zr_copy(2 * k + 1, 8 - 2 * k).start()
+            zr_copy(2 * k + 1, 8 - turn(k)).start()
 
     def when(k, work):
         @pl.when((k >= 0) & (k < CHUNKS))
@@ -438,13 +440,14 @@
     dispatch(0)
 
     def step_of(t, carry):
+        when(t - 1, gather_far)
+        when(t + 0, gather_near)
+        when(t + 1, dispatch)
+        when(t - 2, expert_hidden)
+        when(t - 3, return_near)
+        when(t - 2, expert_out)
+        when(t - 4, return_rows)
         when(t - 5, combine)
-        when(t, gather_near)
-        when(t + 1, dispatch)
-        when(t - 1, gather_far)
-        when(t - 4, return_rows)
-        when(t - 3, return_near)
-        when(t - 2, expert_apply)
         return carry
 
     lax.fori_loop(0, CHUNKS + 5, step_of, 0)

time: 134 us -> 121 us (0.903)
  Pallas kernels: 132 us -> 120 us
    pallas_call x1, Pallas kernels: 132 us -> 120 us  [on_device(): pl.pallas_call(kernel, out_shape=jax.ShapeDtypeStruct((8, D), BF16), in_s...]
where the time goes in v3:
time: 121 us
  Pallas kernels  120 us (99%)
  local copies, waits for them, and re-layouts  1.54 us (1%)
    pallas_call x1, Pallas kernels, on_device(): pl.pallas_call(kernel, out_shape=jax.ShapeDtypeStruct((8, D), BF16), in_s...  120 us

profile of v3, /device:TPU:1, one launch (start us, length us, event | category | flops | bytes accessed | tf_op | source)
XLA Modules:
  0.0 121.4 jit_solution(9461366590746177027)
XLA Ops:
  0.0 119.8 %shard_map.82 = bf16[8,6144]{1,0:T(8,128)(2,1)} custom-call(bf16[8,6144]{1,0:T(8,128)(2,1)} %tok_ref.1, f32[1,6144]{1,0:T(1,128)} %bitcast.3, s32[2,8]{1,0:T(2,128)} %bitcast.4, f32[2,8]{1,0:T(2,128)} %bitcast.5, s32[8]{0:T(128)} %cap_ref.1, bf16[1,6144,256]{2,1,0:T(8,128)(2,1)} %wg_ref.1, bf16[1,6144,256]{2,1,0:T(8,128)(2,1)} %wu_ref.1, ...), custom_call_target="tpu_custom_call" | custom-call | tf_op jit(solution)/shard_map/pallas_call | solution.py:506
  119.8 1.5 %copy.10 = bf16[8,6144]{1,0:T(8,128)(2,1)} copy(bf16[8,6144]{1,0:T(8,128)(2,1)} %shard_map.82) | data formatting | bytes 196608

commit v4 on v3

--- a/solution.py
+++ b/solution.py
@@ -13,9 +13,21 @@
 FW = 256
 META = 128
 CHUNKS = 4
-A = 1792
+A = 1664
 B = HALF - A
 TILE = 256
+LOW, HIGH = pl.ds(0, 2), pl.ds(2, 2)
+ORDER = (
+    "d0", "nb0", "nd0", "na0", "d1", "fb0", "fa0", "nb1", "d2", "d3", "nb2", "nd2", "na1", "na2", "fb2", "fb1",
+    "nb3", "nd1", "fa2", "nd3", "fa1", "na3", "h2", "fb3", "fa3", "o2", "h1", "Na2", "o1", "Nc2", "Nb2", "h3", "Ra2",
+    "Na1", "Rb2", "o3", "Nc1", "h0", "Nc3", "Na3", "Ra1", "C2", "Nb1", "Rb1", "o0", "Na0", "C1", "Nb3", "Nc0", "Ra3",
+    "Rb3", "Nb0", "Ra0", "Rb0", "C3", "C0",
+)
+FIRST = 2
+
+
+def tiles_of(width):
+    return [(start, min(TILE, width - start)) for start in range(0, width, TILE)]
 
 
 def device_of(x, y, z, core):
@@ -95,9 +107,6 @@
     own = 1
     TURNS = (0, 2, 4, 6)
 
-    def turn(k):
-        return 2 * k
-
     def place(d):
         return 2 * TURNS.index(d - 1) if d % 2 else 2 * TURNS.index((8 - d) % 8) + 1
 
@@ -190,24 +199,26 @@
         )
 
     def x1_copies(k):
+        def copy(way, turn, rows, device):
+            return remote(
+                xbuf_a.at[k, 0, rows], xbuf_a.at[k, 1 + way, rows], x1_s.at[k, way, turn], x1_r.at[k, way, turn], device
+            )
+
+        return copy(0, 0, LOW, right), copy(1, 0, HIGH, left), copy(0, 1, HIGH, right), copy(1, 1, LOW, left)
+
+    def x2_copies(k):
         return (
-            remote(xbuf_a.at[k, 0], xbuf_a.at[k, 1], x1_s.at[k, 0], x1_r.at[k, 0], right),
-            remote(xbuf_a.at[k, 0], xbuf_a.at[k, 2], x1_s.at[k, 1], x1_r.at[k, 1], left),
+            remote(xbuf_a.at[k, 1, LOW], xbuf_a.at[k, 3, LOW], x2_s.at[k, 0], x2_r.at[k, 0], right),
+            remote(xbuf_a.at[k, 2, HIGH], xbuf_a.at[k, 3, HIGH], x2_s.at[k, 1], x2_r.at[k, 1], left),
         )
 
-    def x2_copies(k):
-        low, high = pl.ds(0, 2), pl.ds(2, 2)
-        return (
-            remote(xbuf_a.at[k, 1, low], xbuf_a.at[k, 3, low], x2_s.at[k, 0], x2_r.at[k, 0], right),
-            remote(xbuf_a.at[k, 2, high], xbuf_a.at[k, 3, high], x2_s.at[k, 1], x2_r.at[k, 1], left),
-        )
-
     def b1_copies(k):
-        source = ztok.at[pl.ds(2 * k, 2), :, A:]
-        return (
-            remote(source, xtok.at[k, 0], b1_s.at[k, 0], b1_r.at[k, 0], right),
-            remote(source, xtok.at[k, 1], b1_s.at[k, 1], b1_r.at[k, 1], left),
-        )
+        def copy(way, turn, n, device):
+            return remote(
+                ztok.at[2 * k + n, :, A:], xtok.at[k, way, n], b1_s.at[k, way, turn], b1_r.at[k, way, turn], device
+            )
+
+        return copy(0, 0, 0, right), copy(1, 0, 1, left), copy(0, 1, 1, right), copy(1, 1, 0, left)
 
     def b2_copies(k):
         return (
@@ -218,46 +229,50 @@
     def dispatch(k):
         z_arrival(2 * k).wait_recv()
 
-        @pl.when(k > 0)
-        def _():
+        if k > 0:
             z_arrival(2 * k + 1).wait_recv()
-
         for copy in b1_copies(k):
             copy.start()
         picker = picker_of(ztok[pl.ds(2 * k, 2), :, HALF:].reshape(32, META))
 
-        def slots_at(start):
-            return picked(picker, ztok[pl.ds(2 * k, 2), :, start : start + TILE].reshape(32, TILE))
-
-        for start in range(0, A, TILE):
-            slots = slots_at(start)
-            xbuf_a[k, 0, 0, :, start : start + TILE] = slots[0]
-            sbuf_a[k, :, :, start : start + TILE] = slots[1:]
+        def slots_at(start, width):
+            return picked(picker, ztok[pl.ds(2 * k, 2), :, start : start + width].reshape(32, width))
+
+        for start, width in tiles_of(A):
+            slots = slots_at(start, width)
+            xbuf_a[k, 0, 0, :, start : start + width] = slots[0]
+            sbuf_a[k, :, :, start : start + width] = slots[1:]
         for r in (2, 1, 3):
             ya_copy(k, r).start()
-        for start in range(0, B, TILE):
-            slots = slots_at(A + start)
-            xbuf_b[k, 0, 0, :, start : start + TILE] = slots[0]
-            sbuf_b[k, :, 0, :, start : start + TILE] = slots[1:]
+        for start, width in tiles_of(B):
+            slots = slots_at(A + start, width)
+            xbuf_b[k, 0, 0, :, start : start + width] = slots[0]
+            sbuf_b[k, :, 0, :, start : start + width] = slots[1:]
         for r in (2, 1, 3):
             yb_copy(k, 0, r).start()
 
     def dispatch_from(k, rel):
         picker = picker_of(xtok[k, rel - 1, :, :, B:].reshape(32, META))
-        for start in range(0, B, TILE):
-            slots = picked(picker, xtok[k, rel - 1, :, :, start : start + TILE].reshape(32, TILE))
-            xbuf_b[k, rel, 0, :, start : start + TILE] = slots[0]
-            sbuf_b[k, :, rel, :, start : start + TILE] = slots[1:]
-
-    def gather_near(k):
+        for start, width in tiles_of(B):
+            slots = picked(picker, xtok[k, rel - 1, :, :, start : start + width].reshape(32, width))
+            xbuf_b[k, rel, 0, :, start : start + width] = slots[0]
+            sbuf_b[k, :, rel, :, start : start + width] = slots[1:]
+
+    def pass_tokens(k):
         for near, far in zip(b1_copies(k), b2_copies(k)):
             near.wait_recv()
             far.start()
+
+    def ring_slots(k):
         for r in (1, 3, 2):
             ya_copy(k, r).wait_recv()
         for copy in x1_copies(k):
             copy.start()
 
+    def dispatch_near(k):
+        for copy in b1_copies(k)[2:]:
+            copy.wait_recv()
+
         @pl.loop(1, 3)
         def _(rel):
             dispatch_from(k, rel)
@@ -265,12 +280,14 @@
         for r in (2, 1, 3):
             yb_copy(k, 1, r).start()
 
-    def gather_far(k):
+    def dispatch_far(k):
         for copy in b2_copies(k):
             copy.wait_recv()
         dispatch_from(k, 3)
         for r in (2, 1, 3):
             yb_copy(k, 2, r).start()
+
+    def pass_slots(k):
         for near, far in zip(x1_copies(k), x2_copies(k)):
             near.wait_recv()
             far.start()
@@ -282,23 +299,29 @@
         return remote(hbuf.at[k, 0], hbuf.at[k, 1], h_s.at[k], h_r.at[k], sibling)
 
     def r1_copies(k):
-        low, high = pl.ds(0, 2), pl.ds(2, 2)
         return (
-            remote(ybuf_a.at[k, 3, low], r1buf.at[k, 0], r1_s.at[k, 0], r1_r.at[k, 0], left),
-            remote(ybuf_a.at[k, 3, high], r1buf.at[k, 1], r1_s.at[k, 1], r1_r.at[k, 1], right),
+            remote(ybuf_a.at[k, 3, LOW], r1buf.at[k, 0], r1_s.at[k, 0], r1_r.at[k, 0], left),
+            remote(ybuf_a.at[k, 3, HIGH], r1buf.at[k, 1], r1_s.at[k, 1], r1_r.at[k, 1], right),
         )
 
     def r2_copies(k):
-        return (
-            remote(ybuf_a.at[k, 1], r2buf.at[k, 1], r2_s.at[k, 1], r2_r.at[k, 1], left),
-            remote(ybuf_a.at[k, 2], r2buf.at[k, 0], r2_s.at[k, 0], r2_r.at[k, 0], right),
-        )
+        def copy(way, turn, rows, device):
+            return remote(
+                ybuf_a.at[k, 1 + way, rows], r2buf.at[k, 1 - way, rows], r2_s.at[k, way, turn], r2_r.at[k, way, turn], device
+            )
+
+        return copy(0, 0, HIGH, left), copy(1, 0, LOW, right), copy(0, 1, LOW, left), copy(1, 1, HIGH, right)
 
     def yra_copy(k, i):
         return remote(rbuf.at[k, i - 1], yret_a.at[k, 4 - i], yra_s.at[k, i - 1], yra_r.at[k, 3 - i], at_y(i))
 
-    def yrb_copy(k, i):
-        return remote(ybuf_b.at[k, :, i], yret_b.at[k, :, 3 - i], yrb_s.at[k, i - 1], yrb_r.at[k, 3 - i], at_y(i))
+    RETURNS = ((3, 1), (0, 3))
+
+    def yrb_copy(k, part, i):
+        rows = pl.ds(*RETURNS[part])
+        return remote(
+            ybuf_b.at[k, rows, i], yret_b.at[k, rows, 3 - i], yrb_s.at[k, part, i - 1], yrb_r.at[k, part, 3 - i], at_y(i)
+        )
 
     def t1_copies(k):
         return (
@@ -307,20 +330,20 @@
         )
 
     def t2_copies(k):
-        return (
-            remote(tokb.at[k, 1], t2buf.at[k, 1], t2_s.at[k, 1], t2_r.at[k, 1], left),
-            remote(tokb.at[k, 2], t2buf.at[k, 0], t2_s.at[k, 0], t2_r.at[k, 0], right),
-        )
+        def copy(way, turn, n, device):
+            return remote(
+                tokb.at[k, 1 + way, n], t2buf.at[k, 1 - way, n], t2_s.at[k, way, turn], t2_r.at[k, way, turn], device
+            )
+
+        return copy(0, 0, 1, left), copy(1, 0, 0, right), copy(0, 1, 0, left), copy(1, 1, 1, right)
 
     def expert_hidden(k):
-        @pl.when(k == 0)
-        def _():
+        if k == FIRST:
             for copy in local_weights:
                 copy.wait()
             for copy in pair_weights:
                 copy.wait_recv()
-
-        for copy in x2_copies(k):
+        for copy in x1_copies(k)[2:] + x2_copies(k):
             copy.wait_recv()
         for part in range(3):
             for r in (1, 3, 2):
@@ -349,21 +372,20 @@
     def expert_out(k):
         hidden_copy(k).wait_recv()
 
-        def outputs(columns):
+        def outputs(start, width):
+            columns = slice(start, start + width)
             made = jnp.dot(hbuf[k, 0], wdn[0, :, columns], preferred_element_type=F32)
             made = made + jnp.dot(hbuf[k, 1], wdn[1, :, columns], preferred_element_type=F32)
-            return made.astype(BF16).reshape(4, 4, 16, TILE)
-
-        for start in range(0, B, TILE):
-            ybuf_b[k, :, :, :, start : start + TILE] = outputs(slice(A + start, A + start + TILE))
-
-        for i in (2, 1, 3):
-            yrb_copy(k, i).start()
-
-        for start in range(0, A, TILE):
-            ybuf_a[k, :, :, :, start : start + TILE] = outputs(slice(start, start + TILE))
-
-        for copy in r1_copies(k):
+            return made.astype(BF16).reshape(4, 4, 16, width)
+
+        for start, width in tiles_of(B):
+            ybuf_b[k, :, :, :, start : start + width] = outputs(A + start, width)
+        for part in range(2):
+            for i in (2, 1, 3):
+                yrb_copy(k, part, i).start()
+        for start, width in tiles_of(A):
+            ybuf_a[k, :, :, :, start : start + width] = outputs(start, width)
+        for copy in r1_copies(k) + r2_copies(k)[:2]:
             copy.start()
 
     def plus(ref, *others):
@@ -372,39 +394,49 @@
             total = total + term[...].astype(F32)
         return total.astype(BF16)
 
-    def return_near(k):
+    def sum_slots(k):
         for copy in r1_copies(k):
             copy.wait_recv()
         ybuf_a[k, 1, 0:2] = plus(ybuf_a.at[k, 1, 0:2], r1buf.at[k, 0])
         ybuf_a[k, 2, 2:4] = plus(ybuf_a.at[k, 2, 2:4], r1buf.at[k, 1])
-        for copy in r2_copies(k):
+        for copy in r2_copies(k)[2:]:
             copy.start()
+
+    def combine_for(k, rel, meta):
+        weights = weights_of(meta.reshape(32, META), False)
+        for start, width in tiles_of(B):
+            columns = slice(start, start + width)
+            rows = jnp.concatenate([ybuf_b[k, rel, 0, :, columns][None], yret_b[k, rel, :, :, columns]], axis=0)
+            tokb[k, rel, :, :, columns] = combined(weights, rows.reshape(64, width))
+
+    def combine_far(k):
         for i in (1, 3, 2):
-            yrb_copy(k, i).wait_recv()
-
-        def combine_for(rel, meta):
-            weights = weights_of(meta.reshape(32, META), False)
-            for start in range(0, B, TILE):
-                columns = slice(start, start + TILE)
-                rows = jnp.concatenate([ybuf_b[k, rel, 0, :, columns][None], yret_b[k, rel, :, :, columns]], axis=0)
-                tokb[k, rel, :, :, columns] = combined(weights, rows.reshape(64, TILE))
-
-        combine_for(3, xtok[k, 2, :, :, B:])
+            yrb_copy(k, 0, i).wait_recv()
+        combine_for(k, 3, xtok[k, 2, :, :, B:])
         for copy in t1_copies(k):
             copy.start()
-        combine_for(0, ztok[pl.ds(2 * k, 2), :, HALF:])
+
+    def combine_near(k):
+        for i in (1, 3, 2):
+            yrb_copy(k, 1, i).wait_recv()
 
         @pl.loop(1, 3)
         def _(rel):
-            combine_for(rel, xtok[k, rel - 1, :, :, B:])
-
-    def return_rows(k):
+            combine_for(k, rel, xtok[k, rel - 1, :, :, B:])
+
+        for copy in t2_copies(k)[:2]:
+            copy.start()
+        combine_for(k, 0, ztok[pl.ds(2 * k, 2), :, HALF:])
+
+    def sum_tokens(k):
         for copy in t1_copies(k):
             copy.wait_recv()
         tokb[k, 1, 0] = plus(tokb.at[k, 1, 0], t1buf.at[k, 0])
         tokb[k, 2, 1] = plus(tokb.at[k, 2, 1], t1buf.at[k, 1])
-        for copy in t2_copies(k):
+        for copy in t2_copies(k)[2:]:
             copy.start()
+
+    def return_slots(k):
         for copy in r2_copies(k):
             copy.wait_recv()
         total = plus(ybuf_a.at[k, 0], r2buf.at[k, 0], r2buf.at[k, 1])
@@ -423,34 +455,31 @@
         for r in (1, 3, 2):
             yra_copy(k, r).wait_recv()
         weights = weights_of(ztok[pl.ds(2 * k, 2), :, HALF:].reshape(32, META), False)
-        for start in range(0, A, TILE):
-            columns = slice(start, start + TILE)
-            zsend[pl.ds(2 * k, 2), :, columns] = combined(weights, yret_a[k, :, :, columns].reshape(64, TILE))
-        zr_copy(2 * k, turn(k) + 1).start()
-
-        @pl.when(k > 0)
-        def _():
-            zr_copy(2 * k + 1, 8 - turn(k)).start()
-
-    def when(k, work):
-        @pl.when((k >= 0) & (k < CHUNKS))
-        def _():
-            work(k)
-
-    dispatch(0)
-
-    def step_of(t, carry):
-        when(t - 1, gather_far)
-        when(t + 0, gather_near)
-        when(t + 1, dispatch)
-        when(t - 2, expert_hidden)
-        when(t - 3, return_near)
-        when(t - 2, expert_out)
-        when(t - 4, return_rows)
-        when(t - 5, combine)
-        return carry
-
-    lax.fori_loop(0, CHUNKS + 5, step_of, 0)
+        for start, width in tiles_of(A):
+            columns = slice(start, start + width)
+            zsend[pl.ds(2 * k, 2), :, columns] = combined(weights, yret_a[k, :, :, columns].reshape(64, width))
+        zr_copy(2 * k, TURNS[k] + 1).start()
+        if k > 0:
+            zr_copy(2 * k + 1, 8 - TURNS[k]).start()
+
+    stages = {
+        "d": dispatch,
+        "nb": pass_tokens,
+        "na": ring_slots,
+        "nd": dispatch_near,
+        "fb": dispatch_far,
+        "fa": pass_slots,
+        "h": expert_hidden,
+        "o": expert_out,
+        "Na": sum_slots,
+        "Nc": combine_far,
+        "Nb": combine_near,
+        "Rb": sum_tokens,
+        "Ra": return_slots,
+        "C": combine,
+    }
+    for name in ORDER:
+        stages[name[:-1]](int(name[-1]))
 
     total = zsend[own].astype(F32)
     for n in (0, 2, 3, 4, 5, 6, 7):
@@ -479,7 +508,8 @@
         for r in (1, 2, 3):
             ya_copy(k, r).wait_send()
             yra_copy(k, r).wait_send()
-            yrb_copy(k, r).wait_send()
+            for part in range(2):
+                yrb_copy(k, part, r).wait_send()
             for part in range(3):
                 yb_copy(k, part, r).wait_send()
         for copies in (x1_copies, x2_copies, b1_copies, b2_copies, r1_copies, r2_copies, t1_copies, t2_copies):
@@ -542,11 +572,12 @@
         + sems(8) * 2
         + sems(k, 3) * 2
         + sems(k, 3, 3) * 2
-        + sems(k, 2) * 8
+        + (sems(k, 2, 2) * 2 + sems(k, 2) * 2) * 2
         + sems(3) * 3
         + sems(k) * 4
-        + sems(k, 2) * 8
-        + sems(k, 3) * 4
+        + (sems(k, 2) * 2 + sems(k, 2, 2) * 2) * 2
+        + sems(k, 3) * 2
+        + sems(k, 2, 3) * 2
         + sems(8) * 2
         + sems(2),
         compiler_params=pltpu.CompilerParams(

time: 121 us -> 117 us (0.967)
  Pallas kernels: 120 us -> 115 us
    pallas_call x1, Pallas kernels: 120 us -> 115 us  [on_device(): pl.pallas_call(kernel, out_shape=jax.ShapeDtypeStruct((8, D), BF16), in_s...]
where the time goes in v4:
time: 117 us
  Pallas kernels  115 us (98%)
  local copies, waits for them, and re-layouts  1.54 us (1%)
    pallas_call x1, Pallas kernels, on_device(): pl.pallas_call(kernel, out_shape=jax.ShapeDtypeStruct((8, D), BF16), in_s...  115 us

profile of v4, /device:TPU:1, one launch (start us, length us, event | category | flops | bytes accessed | tf_op | source)
XLA Modules:
  0.0 116.8 jit_solution(14092469032444293527)
XLA Ops:
  0.0 115.2 %shard_map.82 = bf16[8,6144]{1,0:T(8,128)(2,1)} custom-call(bf16[8,6144]{1,0:T(8,128)(2,1)} %tok_ref.1, f32[1,6144]{1,0:T(1,128)} %bitcast.3, s32[2,8]{1,0:T(2,128)} %bitcast.4, f32[2,8]{1,0:T(2,128)} %bitcast.5, s32[8]{0:T(128)} %cap_ref.1, bf16[1,6144,256]{2,1,0:T(8,128)(2,1)} %wg_ref.1, bf16[1,6144,256]{2,1,0:T(8,128)(2,1)} %wu_ref.1, ...), custom_call_target="tpu_custom_call" | custom-call | tf_op jit(solution)/shard_map/pallas_call | solution.py:536
  115.2 1.5 %copy.10 = bf16[8,6144]{1,0:T(8,128)(2,1)} copy(bf16[8,6144]{1,0:T(8,128)(2,1)} %shard_map.82) | data formatting | bytes 196608

commit v5 on v4

--- a/solution.py
+++ b/solution.py
@@ -77,12 +77,13 @@
 
 
 def kernel(
-    tok_ref, gain_ref, routes_ref, gates_ref, cap_ref, wg_ref, wu_ref, wd_ref, out_ref,
+    tok_hbm, gain_hbm, routes_hbm, gates_hbm, cap_hbm, wg_ref, wu_ref, wd_ref, out_ref,
+    tok_ref, gain_ref, routes_ref, gates_ref, cap_ref,
     pair_src, pair_dst, ztok, sbuf_a, sbuf_b, xtok, xbuf_a, xbuf_b, wgu, wdn, gsend, grecv, gown, hbuf,
-    ybuf_a, ybuf_b, r1buf, r2buf, rbuf, yret_a, yret_b, tokb, t1buf, t2buf, zsend, zret, fin_src, fin_dst,
+    ybuf_a, ybuf_b, r1buf, r2buf, rbuf, yret_a, yret_b, tokb, t1buf, t2buf, zsend, zret,
     pair_sem, z_s, z_r, ya_s, ya_r, yb_s, yb_r, x1_s, x1_r, x2_s, x2_r, b1_s, b1_r, b2_s, b2_r,
     w_l, w_s, w_r, g_s, g_r, h_s, h_r, r1_s, r1_r, r2_s, r2_r, t1_s, t1_r, t2_s, t2_r,
-    yra_s, yra_r, yrb_s, yrb_r, zr_s, zr_r, fin_sem,
+    yra_s, yra_r, yrb_s, yrb_r, zr_s, zr_r, in_sem,
 ):
     me_e, me_s = lax.axis_index("expert"), lax.axis_index("shard")
     z_lo, y = me_e // 4, lax.rem(me_e, 4)
@@ -96,13 +97,23 @@
     def at_y(r):
         return device_of(x, lax.rem(y + r, 4), z, core)
 
-    def at_z(d):
-        return device_of(x, y, lax.rem(z + d, 8), core)
+    def at_z(d, to_core=core):
+        return device_of(x, y, lax.rem(z + d, 8), to_core)
 
     barrier = pltpu.get_barrier_semaphore()
-    greeted = [at_z(d) for d in (4, 3, 5, 2, 6, 1, 7)] + [at_y(r) for r in (2, 1, 3)] + [left, right, sibling]
+    greeted = [at_z(d, c) for d in (4, 3, 5, 2, 6, 1, 7) for c in (0, 1)] + [at_y(r) for r in (2, 1, 3)] + [left, right, sibling]
     for device in greeted:
         pl.semaphore_signal(barrier, inc=1, device_id=device, device_id_type=MESH)
+
+    inputs = [
+        pltpu.make_async_copy(tok_hbm, tok_ref, in_sem.at[0]),
+        pltpu.make_async_copy(gain_hbm, gain_ref, in_sem.at[1]),
+        pltpu.make_async_copy(routes_hbm, routes_ref, in_sem.at[2]),
+        pltpu.make_async_copy(gates_hbm, gates_ref, in_sem.at[3]),
+        pltpu.make_async_copy(cap_hbm, cap_ref, in_sem.at[4]),
+    ]
+    for copy in inputs:
+        copy.start()
 
     own = 1
     TURNS = (0, 2, 4, 6)
@@ -125,6 +136,8 @@
     for copy in local_weights:
         copy.start()
 
+    for copy in inputs:
+        copy.wait()
     tokens = tok_ref[...].astype(F32)
     scale = lax.rsqrt(jnp.mean(tokens * tokens, axis=-1, keepdims=True) + 1e-05)
     normed = tokens * scale * gain_ref[...]
@@ -185,7 +198,7 @@
         high = weights.astype(BF16)
         rest = (weights - high.astype(F32)).astype(BF16)
         made = jnp.dot(high, rows, preferred_element_type=F32) + jnp.dot(rest, rows, preferred_element_type=F32)
-        return made.astype(BF16).reshape(2, 16, rows.shape[1])
+        return made
 
     def ya_copy(k, r):
         return remote(sbuf_a.at[k, r - 1], xbuf_a.at[k, 0, 4 - r], ya_s.at[k, r - 1], ya_r.at[k, 3 - r], at_y(r))
@@ -407,7 +420,7 @@
         for start, width in tiles_of(B):
             columns = slice(start, start + width)
             rows = jnp.concatenate([ybuf_b[k, rel, 0, :, columns][None], yret_b[k, rel, :, :, columns]], axis=0)
-            tokb[k, rel, :, :, columns] = combined(weights, rows.reshape(64, width))
+            tokb[k, rel, :, :, columns] = combined(weights, rows.reshape(64, width)).astype(BF16).reshape(2, 16, width)
 
     def combine_far(k):
         for i in (1, 3, 2):
@@ -445,22 +458,35 @@
         for i in (2, 1, 3):
             yra_copy(k, i).start()
 
-    def zr_copy(n, d):
-        return remote(zsend.at[n], zret.at[n], zr_s.at[n], zr_r.at[n], at_z(d))
+    def zr_copy(n, d, c):
+        return remote(zsend.at[n, c], zret.at[n, core], zr_s.at[n, c], zr_r.at[n, core], at_z(d, c))
+
+    def zr_sibling():
+        return remote(zsend.at[own, 1 - core], zret.at[own, core], zr_s.at[own, 1 - core], zr_r.at[own, core], sibling)
+
+    def zr_arrival(n, h):
+        return remote(zsend.at[n, 0], zret.at[n, h], zr_s.at[n, 0], zr_r.at[n, h], at_z(1))
 
     def combine(k):
         for copy in t2_copies(k):
             copy.wait_recv()
-        zsend[pl.ds(2 * k, 2), :, A:] = plus(tokb.at[k, 0], t2buf.at[k, 0], t2buf.at[k, 1])
+        total = tokb[k, 0].astype(F32) + t2buf[k, 0].astype(F32) + t2buf[k, 1].astype(F32)
+        zsend[pl.ds(2 * k, 2), :, :, A:] = total.reshape(2, 2, 8, B).astype(BF16)
         for r in (1, 3, 2):
             yra_copy(k, r).wait_recv()
         weights = weights_of(ztok[pl.ds(2 * k, 2), :, HALF:].reshape(32, META), False)
         for start, width in tiles_of(A):
             columns = slice(start, start + width)
-            zsend[pl.ds(2 * k, 2), :, columns] = combined(weights, yret_a[k, :, :, columns].reshape(64, width))
-        zr_copy(2 * k, TURNS[k] + 1).start()
+            made = combined(weights, yret_a[k, :, :, columns].reshape(64, width))
+            zsend[pl.ds(2 * k, 2), :, :, columns] = made.reshape(2, 2, 8, width).astype(BF16)
+        for c in (0, 1):
+            zr_copy(2 * k, TURNS[k] + 1, c).start()
         if k > 0:
-            zr_copy(2 * k + 1, 8 - TURNS[k]).start()
+            for c in (0, 1):
+                zr_copy(2 * k + 1, 8 - TURNS[k], c).start()
+        else:
+            zr_sibling().start()
+            zret[own, core] = zsend[own, core]
 
     stages = {
         "d": dispatch,
@@ -481,28 +507,11 @@
     for name in ORDER:
         stages[name[:-1]](int(name[-1]))
 
-    total = zsend[own].astype(F32)
-    for n in (0, 2, 3, 4, 5, 6, 7):
-        zr_copy(n, 1).wait_recv()
-        total = total + zret[n].astype(F32)
-    total = total.astype(BF16).astype(F32)
-    fin_src[...] = jnp.where(first, total[8:], total[:8]).astype(BF16)
-    fin = remote(fin_src, fin_dst, fin_sem.at[0], fin_sem.at[1], sibling)
-    fin.start()
-    kept = jnp.where(first, total[:8], total[8:])
-    fin.wait_recv()
-    theirs = fin_dst[...].astype(F32)
-    out_ref[:, :HALF] = jnp.where(first, kept, theirs).astype(BF16)
-    out_ref[:, HALF:] = jnp.where(first, theirs, kept).astype(BF16)
-
-    fin.wait_send()
     pair.wait_send()
     for copy in pair_weights:
         copy.wait_send()
     for d in range(1, 8):
         z_copy(d).wait_send()
-    for n in (0, 2, 3, 4, 5, 6, 7):
-        zr_copy(n, 1).wait_send()
 
     def sent(k, carry):
         for r in (1, 2, 3):
@@ -521,9 +530,27 @@
 
     lax.fori_loop(0, CHUNKS, sent, 0)
 
+    totals = [jnp.zeros((8, HALF), F32)] * 2
+    for k in [int(name[1:]) for name in ORDER if name[0] == "C"]:
+        for n in (2 * k, 2 * k + 1):
+            if n == own:
+                remote(
+                    zsend.at[own, 0], zret.at[own, 1 - core], zr_s.at[own, 0], zr_r.at[own, 1 - core], sibling
+                ).wait_recv()
+            for h in (0, 1):
+                if n != own:
+                    zr_arrival(n, h).wait_recv()
+                totals[h] = totals[h] + zret[n, h].astype(F32)
+    for h in (0, 1):
+        out_ref[:, h * HALF : (h + 1) * HALF] = totals[h].astype(BF16)
+    zr_sibling().wait_send()
+    for n in (0, 2, 3, 4, 5, 6, 7):
+        for c in (0, 1):
+            zr_copy(n, 1, c).wait_send()
+
 
 def on_device(tokens, norm_gain, routes, gate_weights, capacity, w_gate, w_up, w_down):
-    vmem, smem = pl.BlockSpec(memory_space=pltpu.VMEM), pl.BlockSpec(memory_space=pltpu.SMEM)
+    vmem = pl.BlockSpec(memory_space=pltpu.VMEM)
     whole = pl.BlockSpec(memory_space=pl.ANY)
     k = CHUNKS
 
@@ -536,9 +563,14 @@
     return pl.pallas_call(
         kernel,
         out_shape=jax.ShapeDtypeStruct((8, D), BF16),
-        in_specs=[vmem, vmem, vmem, vmem, smem, whole, whole, whole],
+        in_specs=[whole] * 8,
         out_specs=vmem,
         scratch_shapes=[
+            held(8, D),
+            held(1, D, dtype=F32),
+            held(2, 8, dtype=jnp.int32),
+            held(2, 8, dtype=F32),
+            pltpu.SMEM((8,), jnp.int32),
             held(8, HALF + META),
             held(8, HALF + META),
             held(8, 16, HALF + META),
@@ -563,10 +595,8 @@
             held(k, 4, 2, 16, B),
             held(k, 2, 16, B),
             held(k, 2, 2, 16, B),
-            held(8, 16, HALF),
-            held(8, 16, HALF),
-            held(8, HALF),
-            held(8, HALF),
+            held(8, 2, 8, HALF),
+            held(8, 2, 8, HALF),
         ]
         + sems(2)
         + sems(8) * 2
@@ -578,8 +608,8 @@
         + (sems(k, 2) * 2 + sems(k, 2, 2) * 2) * 2
         + sems(k, 3) * 2
         + sems(k, 2, 3) * 2
-        + sems(8) * 2
-        + sems(2),
+        + sems(8, 2) * 2
+        + sems(5),
         compiler_params=pltpu.CompilerParams(
             collective_id=0, has_side_effects=True, vmem_limit_bytes=67043328
         ),

time: 117 us -> 113 us (0.966)
  Pallas kernels: 115 us -> 112 us
    pallas_call x1, Pallas kernels: 115 us -> 112 us  [on_device(): pl.pallas_call(kernel, out_shape=jax.ShapeDtypeStruct((8, D), BF16), in_s...]
where the time goes in v5:
time: 113 us
  Pallas kernels  112 us (99%)
  local copies, waits for them, and re-layouts  1.54 us (1%)
    pallas_call x1, Pallas kernels, on_device(): pl.pallas_call(kernel, out_shape=jax.ShapeDtypeStruct((8, D), BF16), in_s...  112 us

profile of v5, /device:TPU:1, one launch (start us, length us, event | category | flops | bytes accessed | tf_op | source)
XLA Modules:
  0.0 113.4 jit_solution(15448874882207870220)
XLA Ops:
  0.0 111.8 %shard_map.82 = bf16[8,6144]{1,0:T(8,128)(2,1)} custom-call(bf16[8,6144]{1,0:T(8,128)(2,1)} %tok_hbm.1, f32[1,6144]{1,0:T(1,128)} %bitcast.3, s32[2,8]{1,0:T(2,128)} %bitcast.4, f32[2,8]{1,0:T(2,128)} %bitcast.5, s32[8]{0:T(128)} %cap_hbm.1, bf16[1,6144,256]{2,1,0:T(8,128)(2,1)} %wg_ref.1, bf16[1,6144,256]{2,1,0:T(8,128)(2,1)} %wu_ref.1, ...), custom_call_target="tpu_custom_call" | custom-call | tf_op jit(solution)/shard_map/pallas_call | solution.py:563
  111.8 1.5 %copy.10 = bf16[8,6144]{1,0:T(8,128)(2,1)} copy(bf16[8,6144]{1,0:T(8,128)(2,1)} %shard_map.82) | data formatting | bytes 196608

commit v6 on v5

--- a/solution.py
+++ b/solution.py
@@ -18,10 +18,10 @@
 TILE = 256
 LOW, HIGH = pl.ds(0, 2), pl.ds(2, 2)
 ORDER = (
-    "d0", "nb0", "nd0", "na0", "d1", "fb0", "fa0", "nb1", "d2", "d3", "nb2", "nd2", "na1", "na2", "fb2", "fb1",
-    "nb3", "nd1", "fa2", "nd3", "fa1", "na3", "h2", "fb3", "fa3", "o2", "h1", "Na2", "o1", "Nc2", "Nb2", "h3", "Ra2",
-    "Na1", "Rb2", "o3", "Nc1", "h0", "Nc3", "Na3", "Ra1", "C2", "Nb1", "Rb1", "o0", "Na0", "C1", "Nb3", "Nc0", "Ra3",
-    "Rb3", "Nb0", "Ra0", "Rb0", "C3", "C0",
+    "d0", "nb0", "d1", "nd0", "na0", "nb1", "d2", "fa0", "fb0", "d3", "nb2", "na2", "nd2", "nb3", "fa2", "fb2",
+    "nd3", "na3", "nd1", "na1", "h2", "fb3", "fa3", "fb1", "o2", "fa1", "h0", "h3", "Na2", "Nc2", "o3", "h1", "Nb2",
+    "Rb2", "Nc3", "Na3", "Ra2", "o1", "Nb3", "Ra3", "Rb3", "o0", "Na1", "C2", "Nc1", "C3", "Na0", "Nc0", "Nb1",
+    "Ra1", "Rb1", "Ra0", "Nb0", "Rb0", "C1", "C0",
 )
 FIRST = 2
 
@@ -79,9 +79,9 @@
 def kernel(
     tok_hbm, gain_hbm, routes_hbm, gates_hbm, cap_hbm, wg_ref, wu_ref, wd_ref, out_ref,
     tok_ref, gain_ref, routes_ref, gates_ref, cap_ref,
-    pair_src, pair_dst, ztok, sbuf_a, sbuf_b, xtok, xbuf_a, xbuf_b, wgu, wdn, gsend, grecv, gown, hbuf,
+    ztok_src, ztok, sbuf_a, sbuf_b, xtok, xbuf_a, xbuf_b, wgu, wdn, gsend, grecv, gown, hbuf,
     ybuf_a, ybuf_b, r1buf, r2buf, rbuf, yret_a, yret_b, tokb, t1buf, t2buf, zsend, zret,
-    pair_sem, z_s, z_r, ya_s, ya_r, yb_s, yb_r, x1_s, x1_r, x2_s, x2_r, b1_s, b1_r, b2_s, b2_r,
+    z_s, z_r, ya_s, ya_r, yb_s, yb_r, x1_s, x1_r, x2_s, x2_r, b1_s, b1_r, b2_s, b2_r,
     w_l, w_s, w_r, g_s, g_r, h_s, h_r, r1_s, r1_r, r2_s, r2_r, t1_s, t1_r, t2_s, t2_r,
     yra_s, yra_r, yrb_s, yrb_r, zr_s, zr_r, in_sem,
 ):
@@ -116,7 +116,7 @@
         copy.start()
 
     own = 1
-    TURNS = (0, 2, 4, 6)
+    TURNS = (0, 6, 4, 2)
 
     def place(d):
         return 2 * TURNS.index(d - 1) if d % 2 else 2 * TURNS.index((8 - d) % 8) + 1
@@ -142,35 +142,31 @@
     scale = lax.rsqrt(jnp.mean(tokens * tokens, axis=-1, keepdims=True) + 1e-05)
     normed = tokens * scale * gain_ref[...]
     lanes = routing_lanes(columns_of(routes_ref[...]), columns_of(gates_ref[...]), cap_ref)
-    first = core == 0
-    own_half = jnp.where(first, normed[:, :HALF], normed[:, HALF:])
-    pair_src[:, :HALF] = jnp.where(first, normed[:, HALF:], normed[:, :HALF]).astype(BF16)
-    pair_src[:, HALF:] = lanes.astype(BF16)
+    for c in (0, 1):
+        ztok_src[c, :, :HALF] = normed[:, c * HALF : (c + 1) * HALF].astype(BF16)
+        ztok_src[c, :, HALF:] = lanes.astype(BF16)
+
+    def z_copy(d, c):
+        n = place(d)
+        return remote(ztok_src.at[c], ztok.at[n, core], z_s.at[n, c], z_r.at[n, core], at_z(8 - d, c))
+
+    def z_sibling(slot):
+        return remote(ztok_src.at[1 - core], ztok.at[own, slot], z_s.at[own, 0], z_r.at[own, slot], sibling)
+
+    def z_arrival(n, h):
+        return remote(ztok_src.at[0], ztok.at[n, h], z_s.at[n, 0], z_r.at[n, h], at_z(1))
 
     pl.semaphore_wait(barrier, len(greeted))
-    pair = remote(pair_src, pair_dst, pair_sem.at[0], pair_sem.at[1], sibling)
-    pair.start()
+    z_sibling(core).start()
+    for d in (1, 7, 2, 5, 4, 3, 6):
+        for c in (0, 1):
+            z_copy(d, c).start()
     for copy in pair_weights:
         copy.start()
-    pair.wait_recv()
-    their_half = pair_dst[:, :HALF].astype(F32)
-    their_lanes = pair_dst[:, HALF:].astype(F32)
-    ztok[own, :, :HALF] = jnp.concatenate(
-        [jnp.where(first, own_half, their_half), jnp.where(first, their_half, own_half)], axis=0
-    ).astype(BF16)
-    ztok[own, :, HALF:] = jnp.concatenate(
-        [jnp.where(first, lanes, their_lanes), jnp.where(first, their_lanes, lanes)], axis=0
-    ).astype(BF16)
-
-    def z_copy(d):
-        n = place(d)
-        return remote(ztok.at[own], ztok.at[n], z_s.at[n], z_r.at[n], at_z(8 - d))
-
-    for d in (1, 3, 6, 5, 4, 7, 2):
-        z_copy(d).start()
-
-    def z_arrival(n):
-        return remote(ztok.at[own], ztok.at[n], z_s.at[n], z_r.at[n], at_z(1))
+    ztok[own, core] = ztok_src[core]
+
+    def flat(rows):
+        return rows.astype(F32).reshape(32, rows.shape[-1]).astype(BF16)
 
     def weights_of(meta, turned):
         shape = (64, META) if turned else (META, 64)
@@ -228,7 +224,7 @@
     def b1_copies(k):
         def copy(way, turn, n, device):
             return remote(
-                ztok.at[2 * k + n, :, A:], xtok.at[k, way, n], b1_s.at[k, way, turn], b1_r.at[k, way, turn], device
+                ztok.at[2 * k + n, :, :, A:], xtok.at[k, way, n], b1_s.at[k, way, turn], b1_r.at[k, way, turn], device
             )
 
         return copy(0, 0, 0, right), copy(1, 0, 1, left), copy(0, 1, 1, right), copy(1, 1, 0, left)
@@ -240,16 +236,19 @@
         )
 
     def dispatch(k):
-        z_arrival(2 * k).wait_recv()
-
+        for h in (0, 1):
+            z_arrival(2 * k, h).wait_recv()
         if k > 0:
-            z_arrival(2 * k + 1).wait_recv()
+            for h in (0, 1):
+                z_arrival(2 * k + 1, h).wait_recv()
+        else:
+            z_sibling(1 - core).wait_recv()
         for copy in b1_copies(k):
             copy.start()
-        picker = picker_of(ztok[pl.ds(2 * k, 2), :, HALF:].reshape(32, META))
+        picker = picker_of(flat(ztok[pl.ds(2 * k, 2), :, :, HALF:]))
 
         def slots_at(start, width):
-            return picked(picker, ztok[pl.ds(2 * k, 2), :, start : start + width].reshape(32, width))
+            return picked(picker, flat(ztok[pl.ds(2 * k, 2), :, :, start : start + width]))
 
         for start, width in tiles_of(A):
             slots = slots_at(start, width)
@@ -265,9 +264,9 @@
             yb_copy(k, 0, r).start()
 
     def dispatch_from(k, rel):
-        picker = picker_of(xtok[k, rel - 1, :, :, B:].reshape(32, META))
+        picker = picker_of(flat(xtok[k, rel - 1, :, :, :, B:]))
         for start, width in tiles_of(B):
-            slots = picked(picker, xtok[k, rel - 1, :, :, start : start + width].reshape(32, width))
+            slots = picked(picker, flat(xtok[k, rel - 1, :, :, :, start : start + width]))
             xbuf_b[k, rel, 0, :, start : start + width] = slots[0]
             sbuf_b[k, :, rel, :, start : start + width] = slots[1:]
 
@@ -416,7 +415,7 @@
             copy.start()
 
     def combine_for(k, rel, meta):
-        weights = weights_of(meta.reshape(32, META), False)
+        weights = weights_of(flat(meta), False)
         for start, width in tiles_of(B):
             columns = slice(start, start + width)
             rows = jnp.concatenate([ybuf_b[k, rel, 0, :, columns][None], yret_b[k, rel, :, :, columns]], axis=0)
@@ -425,7 +424,7 @@
     def combine_far(k):
         for i in (1, 3, 2):
             yrb_copy(k, 0, i).wait_recv()
-        combine_for(k, 3, xtok[k, 2, :, :, B:])
+        combine_for(k, 3, xtok[k, 2, :, :, :, B:])
         for copy in t1_copies(k):
             copy.start()
 
@@ -435,11 +434,11 @@
 
         @pl.loop(1, 3)
         def _(rel):
-            combine_for(k, rel, xtok[k, rel - 1, :, :, B:])
+            combine_for(k, rel, xtok[k, rel - 1, :, :, :, B:])
 
         for copy in t2_copies(k)[:2]:
             copy.start()
-        combine_for(k, 0, ztok[pl.ds(2 * k, 2), :, HALF:])
+        combine_for(k, 0, ztok[pl.ds(2 * k, 2), :, :, HALF:])
 
     def sum_tokens(k):
         for copy in t1_copies(k):
@@ -474,7 +473,7 @@
         zsend[pl.ds(2 * k, 2), :, :, A:] = total.reshape(2, 2, 8, B).astype(BF16)
         for r in (1, 3, 2):
             yra_copy(k, r).wait_recv()
-        weights = weights_of(ztok[pl.ds(2 * k, 2), :, HALF:].reshape(32, META), False)
+        weights = weights_of(flat(ztok[pl.ds(2 * k, 2), :, :, HALF:]), False)
         for start, width in tiles_of(A):
             columns = slice(start, start + width)
             made = combined(weights, yret_a[k, :, :, columns].reshape(64, width))
@@ -507,11 +506,12 @@
     for name in ORDER:
         stages[name[:-1]](int(name[-1]))
 
-    pair.wait_send()
+    z_sibling(core).wait_send()
     for copy in pair_weights:
         copy.wait_send()
     for d in range(1, 8):
-        z_copy(d).wait_send()
+        for c in (0, 1):
+            z_copy(d, c).wait_send()
 
     def sent(k, carry):
         for r in (1, 2, 3):
@@ -571,12 +571,11 @@
             held(2, 8, dtype=jnp.int32),
             held(2, 8, dtype=F32),
             pltpu.SMEM((8,), jnp.int32),
-            held(8, HALF + META),
-            held(8, HALF + META),
-            held(8, 16, HALF + META),
+            held(2, 8, HALF + META),
+            held(8, 2, 8, HALF + META),
             held(k, 3, 16, A),
             held(k, 3, 4, 16, B),
-            held(k, 3, 2, 16, B + META),
+            held(k, 3, 2, 2, 8, B + META),
             held(k, 4, 4, 16, A),
             held(k, 4, 4, 16, B),
             held(4, HALF, FW),
@@ -598,8 +597,7 @@
             held(8, 2, 8, HALF),
             held(8, 2, 8, HALF),
         ]
-        + sems(2)
-        + sems(8) * 2
+        + sems(8, 2) * 2
         + sems(k, 3) * 2
         + sems(k, 3, 3) * 2
         + (sems(k, 2, 2) * 2 + sems(k, 2) * 2) * 2

time: 113 us -> 111 us (0.982)
  Pallas kernels: 112 us -> 110 us
    pallas_call x1, Pallas kernels: 112 us -> 110 us  [on_device(): pl.pallas_call(kernel, out_shape=jax.ShapeDtypeStruct((8, D), BF16), in_s...]
where the time goes in v6:
time: 111 us
  Pallas kernels  110 us (99%)
  local copies, waits for them, and re-layouts  1.54 us (1%)
    pallas_call x1, Pallas kernels, on_device(): pl.pallas_call(kernel, out_shape=jax.ShapeDtypeStruct((8, D), BF16), in_s...  110 us

profile of v6, /device:TPU:1, one launch (start us, length us, event | category | flops | bytes accessed | tf_op | source)
XLA Modules:
  0.0 111.3 jit_solution(9321041969518076867)
XLA Ops:
  0.0 109.8 %shard_map.82 = bf16[8,6144]{1,0:T(8,128)(2,1)} custom-call(bf16[8,6144]{1,0:T(8,128)(2,1)} %tok_hbm.1, f32[1,6144]{1,0:T(1,128)} %bitcast.3, s32[2,8]{1,0:T(2,128)} %bitcast.4, f32[2,8]{1,0:T(2,128)} %bitcast.5, s32[8]{0:T(128)} %cap_hbm.1, bf16[1,6144,256]{2,1,0:T(8,128)(2,1)} %wg_ref.1, bf16[1,6144,256]{2,1,0:T(8,128)(2,1)} %wu_ref.1, ...), custom_call_target="tpu_custom_call" | custom-call | tf_op jit(solution)/shard_map/pallas_call | solution.py:563
  109.8 1.5 %copy.10 = bf16[8,6144]{1,0:T(8,128)(2,1)} copy(bf16[8,6144]{1,0:T(8,128)(2,1)} %shard_map.82) | data formatting | bytes 196608
